TPU v7x, 512 devices: a whole 4x8x8 slice. The times are simulated.
512 devices in a mesh: slab: 64 (over z, x, core), tile: 8 (over y).
Axes of the slice: x: 4, y: 8, z: 8, core: 2. Of those that a mesh axis runs over, the one named last changes fastest.
Arguments:
- features: bfloat16 [64, 8, 512, 128], P('slab', 'tile'), may hold values from -24 to 24
- counts: int32 [64, 8], P('slab', 'tile'), may hold values from 128 to 512, as said below
- rulebook: int32 [64, 8, 27, 512], P('slab', 'tile'), may hold values from 0 to 800, as said below
- face_rows: int32 [64, 8, 4, 64], P('slab', 'tile'), may hold values from 0 to 511, as said below
- conv_one: bfloat16 [27, 128, 128], replicated, may hold values from -0.109375 to 0.109375
- gain_one: float32 [128], replicated, may hold values from 0.5 to 1.5
- shift_one: float32 [128], replicated, may hold values from -0.5 to 0.5
- conv_two: bfloat16 [27, 128, 128], replicated, may hold values from -0.109375 to 0.109375
- gain_two: float32 [128], replicated, may hold values from 0.5 to 1.5
- shift_two: float32 [128], replicated, may hold values from -0.5 to 0.5
Outputs:
- output: bfloat16 [64, 8, 512, 128], P('slab', 'tile')
Inputs may be any that keep to these rules, and one draw needn't show every extreme that they name: `counts`: each device's voxels fill its 8 x 8 grid columns with the same number each, between 2 and 8; some device of the highest slab index holds 512. `rulebook`: an entry names the extended-table row that holds the voxel's neighbour at offset k = 9 (dx + 1) + 3 (dy + 1) + (dz + 1) of the submanifold 3x3x3 stencil, or 800 where that cell is inactive or outside the grid; the voxel itself is at offset 13; rows at or past the device's count name 800 at every offset. `face_rows`: lists 0 to 3 hold the device's voxels on its lower and higher face along the first, then the lower and higher face along the second dimension; the j-th voxel of the i-th column along a face stands at position i * 8 + j; unused positions name row 0.
All inputs are finite; a program needn't handle non-finite values.
Results may differ from a plain program's by a relative error of at most 0.0033.
Values may be sent and summed in bfloat16 or wider, within the bound.
No kernel may reach another device: no remote copies, remote signals or barrier semaphores. Data moves between devices by JAX's collectives and lax.ppermute only.
A program may use at most 64 MiB of HBM per device.

v0:
```python
import jax
import jax.numpy as jnp
from jax import lax
from jax.experimental import pallas as pl
from jax.experimental.pallas import tpu as pltpu
from jax.sharding import Mesh
from jax.sharding import PartitionSpec as P

ROWS = 512
CH = 128
TAPS = 27
SIDES = 26
CENTRE = 13
SLOTS = 24
DIGIT = 32
TABLE = 800
FACE = 64
COLUMN = 8
SIDE_ROWS = FACE + 2 * COLUMN
HALO = 2 * FACE + 2 * SIDE_ROWS
EXT = 832
SLAB = ("slab_0", "slab_1", "slab_2")
EPSILON = 1e-05


A, B, QH, QL = ROWS, ROWS + FACE, ROWS + 2 * FACE, ROWS + 2 * FACE + SIDE_ROWS


def dot(a, b, **kw):
    return jnp.dot(a, b, preferred_element_type=jnp.float32, **kw)


def hot(index, shape, dim):
    return jnp.where(jnp.broadcast_to(index, shape) == lax.broadcasted_iota(jnp.int32, shape, dim), 1.0, 0.0).astype(
        jnp.bfloat16
    )


def fetch(pairs, sems):
    copies = [pltpu.make_async_copy(src, dst, sems.at[i]) for i, (src, dst) in enumerate(pairs)]
    for copy in copies:
        copy.start()
    return copies


def thirds(values):
    high = values.astype(jnp.bfloat16)
    rest = values - high.astype(jnp.float32)
    mid = rest.astype(jnp.bfloat16)
    return high, mid, (rest - mid.astype(jnp.float32)).astype(jnp.bfloat16)


def face_hot(faces_ref, k):
    return hot(jnp.concatenate([faces_ref[k : k + 1, :], faces_ref[k + 1 : k + 2, :]], axis=1), (ROWS, 2 * FACE), 0)


def pick(selector, rows):
    got = lax.dot_general(
        selector, jnp.concatenate(thirds(rows), axis=1), (((0,), (0,)), ((), ())), preferred_element_type=jnp.float32
    )
    return got[:, :CH] + got[:, CH : 2 * CH] + got[:, 2 * CH :]


def put(selector, values):
    return dot(jnp.concatenate([selector] * 3, axis=1), jnp.concatenate(thirds(values), axis=0))


def plan_pairs(rb_ref, work_ref, rank_ref, rank_t_ref, digits_ref):
    work_ref[...] = jnp.full_like(work_ref, TABLE)
    for t in range(SIDES):
        work_ref[t : t + 1, :] = rb_ref[t + (t >= CENTRE)]
    entry = work_ref[...]
    present = entry != TABLE
    ones = jnp.where(present, 1.0, 0.0)
    before = lax.broadcasted_iota(jnp.int32, (ROWS, ROWS), 0) < lax.broadcasted_iota(jnp.int32, (ROWS, ROWS), 1)
    place = dot(ones.astype(jnp.bfloat16), jnp.where(before, 1.0, 0.0).astype(jnp.bfloat16))
    rank = jnp.where(present, place.astype(jnp.int32), -1)
    rank_ref[...] = rank
    itself = jnp.broadcast_to(jnp.where(rb_ref[CENTRE] != TABLE, 1, -1), (8, ROWS))
    padded = jnp.concatenate([rank, itself, jnp.full((CH - 40, ROWS), -1, jnp.int32)], axis=0)
    rank_t_ref[...] = padded.T
    digits_ref[...] = jnp.concatenate(
        [(entry // DIGIT).astype(jnp.float32), (entry % DIGIT).astype(jnp.float32),
         jnp.zeros((CH - 2 * entry.shape[0], ROWS), jnp.float32)], axis=0
    ).astype(jnp.bfloat16)
    most = jnp.max(jnp.sum(ones, axis=1, keepdims=True))
    return (most.astype(jnp.int32) + (SLOTS - 1)) // SLOTS


def slots_of_rows(rank_ref, base, to_slot_ref):
    slot = lax.broadcasted_iota(jnp.int32, (SLOTS, ROWS), 0) + base
    blocks = []
    for t in range(SIDES):
        match = jnp.broadcast_to(rank_ref[t : t + 1, :], (SLOTS, ROWS)) == slot
        blocks.append(jnp.where(match, 1.0, 0.0))
    to_slot_ref[...] = jnp.concatenate(blocks, axis=0).astype(jnp.bfloat16)


def tap_of_slot(slot):
    return jnp.right_shift(slot * 2731, 16)


def rows_of_slots(rank_t_ref, base, to_row_ref):
    for i in range(to_row_ref.shape[1] // CH):
        slot = lax.broadcasted_iota(jnp.int32, (1, CH), 1) + i * CH
        tap = tap_of_slot(slot)
        wanted = jnp.broadcast_to(slot - tap * SLOTS + base, (ROWS, CH))
        spread = jnp.take_along_axis(
            rank_t_ref[...], jnp.broadcast_to(tap, (ROWS, CH)), axis=1, mode="promise_in_bounds"
        )
        to_row_ref[:, i * CH : (i + 1) * CH] = jnp.where(spread == wanted, 1.0, 0.0).astype(jnp.bfloat16)


def multiply_slots(picked, weight_ref, tap_of, part_ref):
    parts = [
        dot(picked[t * SLOTS : (t + 1) * SLOTS].astype(jnp.bfloat16), weight_ref[tap_of(t)]) for t in range(SIDES)
    ]
    part = jnp.concatenate(parts, axis=0)
    high = part.astype(jnp.bfloat16)
    part_ref[: SIDES * SLOTS, :CH] = high
    part_ref[: SIDES * SLOTS, CH:] = (part - high.astype(jnp.float32)).astype(jnp.bfloat16)


def clear_padding(part_ref):
    part_ref[SIDES * SLOTS :, :] = jnp.zeros((part_ref.shape[0] - SIDES * SLOTS, 2 * CH), jnp.bfloat16)


def spread_kernel(*refs):
    rb_hbm, rows_hbm, weight_hbm, faces_hbm, *params_hbm = refs[:9]
    out_ref, up_ref, down_ref, rank_ref, rank_t_ref, digits_ref, meta_ref, rows_ref, faces_ref, *params = refs[9:23]
    rb_ref, weight_ref, work_ref, to_slot_ref, to_row_ref, part_ref, sems = refs[23:]
    rb_copy, rows_copy, weight_copy, *others = fetch(
        [(rb_hbm, rb_ref), (rows_hbm, rows_ref), (weight_hbm, weight_ref), (faces_hbm, faces_ref),
         *zip(params_hbm, params, strict=True)], sems,
    )
    rb_copy.wait()
    chunks = plan_pairs(rb_ref, work_ref, rank_ref, rank_t_ref, digits_ref)
    present = jnp.where(rb_ref[CENTRE] != TABLE, 1.0, 0.0)
    meta_ref[0:1] = jnp.broadcast_to(jnp.sum(present, axis=1, keepdims=True), (1, CH)).astype(jnp.int32)
    meta_ref[1:2] = jnp.full((1, CH), chunks, jnp.int32)
    clear_padding(part_ref)
    rows_copy.wait()
    weight_copy.wait()
    itself = jnp.broadcast_to(rank_t_ref[:, 32:33], (ROWS, CH)) > 0
    out_ref[:ROWS] = jnp.where(itself, dot(rows_ref[...], weight_ref[CENTRE]), 0.0)
    out_ref[ROWS:] = jnp.zeros((EXT - ROWS, CH), jnp.float32)
    slots = part_ref.shape[0]

    def chunk(c, carry):
        slots_of_rows(rank_ref, c * SLOTS, to_slot_ref)
        picked = dot(to_slot_ref[...], rows_ref[...])
        multiply_slots(picked, weight_ref, lambda t: TAPS - 1 - (t + (t >= CENTRE)), part_ref)
        rows_of_slots(rank_t_ref, c * SLOTS, to_row_ref)
        found = dot(digits_ref[...], to_row_ref[...])
        digit = lax.broadcasted_iota(jnp.int32, (CH, slots), 0)
        tap = jnp.broadcast_to(tap_of_slot(lax.broadcasted_iota(jnp.int32, (1, slots), 1)), (CH, slots))
        worth = jnp.where(digit == tap, float(DIGIT), jnp.where(digit == tap + 32, 1.0, 0.0))
        target = jnp.sum(found * worth, axis=0, keepdims=True).astype(jnp.int32)
        added = dot(hot(target, (EXT, slots), 0), part_ref[...])
        out_ref[...] += added[:, :CH] + added[:, CH:]
        return carry

    lax.fori_loop(0, chunks, chunk, 0)
    for copy in others:
        copy.wait()
    picked = pick(face_hot(faces_ref, 2), out_ref[:ROWS])
    for ref, own, at, far in ((down_ref, picked[:FACE], 0, QH), (up_ref, picked[FACE:], FACE - COLUMN, QL)):
        ref[:COLUMN] = out_ref[A + at : A + at + COLUMN]
        ref[COLUMN : COLUMN + FACE] = own
        ref[COLUMN + FACE : SIDE_ROWS] = out_ref[B + at : B + at + COLUMN]
        ref[SIDE_ROWS:] = out_ref[far : far + SIDE_ROWS]


def tile_kernel(sums_ref, low_ref, high_ref, faces_ref, out_ref, left_ref, right_ref):
    out_ref[...] = sums_ref[...]
    first, last = SIDE_ROWS + COLUMN, SIDE_ROWS + COLUMN + FACE
    out_ref[QH:QL] += low_ref[:SIDE_ROWS]
    out_ref[QL : QL + SIDE_ROWS] += high_ref[:SIDE_ROWS]
    for ref, at in ((low_ref, 0), (high_ref, FACE - COLUMN)):
        out_ref[A + at : A + at + COLUMN] += ref[SIDE_ROWS:first]
        out_ref[B + at : B + at + COLUMN] += ref[last:]
    out_ref[:ROWS] += put(face_hot(faces_ref, 2), jnp.concatenate([low_ref[first:last], high_ref[first:last]], axis=0))
    picked = pick(face_hot(faces_ref, 0), out_ref[:ROWS])
    for ref, own, own_at, far, far_at in (
        (left_ref, picked[:FACE], COLUMN, A, 0),
        (right_ref, picked[FACE:], FACE, B, FACE + COLUMN),
    ):
        ref[:FACE] = own
        ref[SIDE_ROWS : SIDE_ROWS + FACE] = out_ref[far : far + FACE]
        for start, at in ((0, own_at), (SIDE_ROWS, far_at)):
            ref[start + FACE : start + FACE + COLUMN] = out_ref[QH + at : QH + at + COLUMN]
            ref[start + FACE + COLUMN : start + SIDE_ROWS] = out_ref[QL + at : QL + at + COLUMN]


def slab_kernel(meta_ref, sums_ref, low_ref, high_ref, faces_ref, out_ref, stats_ref):
    out_ref[...] = sums_ref[...]
    for ref, far, far_at, own_at in ((low_ref, A, 0, COLUMN), (high_ref, B, FACE + COLUMN, FACE)):
        out_ref[far : far + FACE] += ref[:FACE]
        for start, at in ((0, far_at), (SIDE_ROWS, own_at)):
            out_ref[QH + at : QH + at + COLUMN] += ref[start + FACE : start + FACE + COLUMN]
            out_ref[QL + at : QL + at + COLUMN] += ref[start + FACE + COLUMN : start + SIDE_ROWS]
    own = slice(SIDE_ROWS, SIDE_ROWS + FACE)
    total = out_ref[:ROWS] + put(face_hot(faces_ref, 0), jnp.concatenate([low_ref[own], high_ref[own]], axis=0))
    out_ref[:ROWS] = total
    write_sums(stats_ref, sums_of(total, meta_ref))


def sources(c, rank_ref, digits_ref, to_slot_ref):
    total = SIDES * SLOTS
    slots_of_rows(rank_ref, c * SLOTS, to_slot_ref)
    found = lax.dot_general(
        to_slot_ref[...], digits_ref[...], (((1,), (1,)), ((), ())), preferred_element_type=jnp.float32
    )
    tap = tap_of_slot(lax.broadcasted_iota(jnp.int32, (total, CH), 0))
    lane = lax.broadcasted_iota(jnp.int32, (total, CH), 1)
    worth = jnp.where(lane == tap, float(DIGIT), jnp.where(lane == tap + 32, 1.0, 0.0))
    source = jnp.sum(found * worth, axis=1, keepdims=True).astype(jnp.int32)
    return hot(jnp.bitwise_and(source, ROWS - 1), (total, ROWS), 1), jnp.broadcast_to(source, (total, CH))


def source_kernel(rank_ref, digits_ref, hot_ref, source_ref, to_slot_ref):
    hot_ref[...], source_ref[...] = sources(0, rank_ref, digits_ref, to_slot_ref)


def gather_kernel(
    meta_ref, first_ref, rank_ref, rank_t_ref, digits_ref, hot_ref, source_ref, weight_ref, stats_ref, gain_ref, shift_ref,
    out_ref, sums_ref, table_ref, to_slot_ref, to_row_ref, part_ref,
):
    norm = scale_of(total_of(stats_ref), gain_ref[...], shift_ref[...])
    live = live_rows(meta_ref)

    def act(values):
        return jnp.maximum(affine(values, *norm), 0.0)

    table_ref[:, :CH] = (live * act(first_ref[:ROWS])).astype(jnp.bfloat16)
    table_ref[:HALO, CH:] = act(first_ref[ROWS : ROWS + HALO]).astype(jnp.bfloat16)
    table_ref[HALO:, CH:] = jnp.zeros((ROWS - HALO, CH), jnp.bfloat16)
    out_ref[...] = dot(table_ref[:, :CH], weight_ref[CENTRE]) * live
    clear_padding(part_ref)

    def add(c, selector, source):
        both = dot(selector, table_ref[...])
        picked = jnp.where(source >= ROWS, both[:, CH:], both[:, :CH])
        multiply_slots(picked, weight_ref, lambda t: t + (t >= CENTRE), part_ref)
        rows_of_slots(rank_t_ref, c * SLOTS, to_row_ref)
        added = dot(to_row_ref[...], part_ref[...])
        out_ref[...] += added[:, :CH] + added[:, CH:]

    def chunk(c, carry):
        add(c, *sources(c, rank_ref, digits_ref, to_slot_ref))
        return carry

    add(0, hot_ref[...], source_ref[...])
    lax.fori_loop(1, jnp.max(meta_ref[1:2]), chunk, 0)
    write_sums(sums_ref, sums_of(out_ref[...], meta_ref))


def live_rows(meta_ref):
    rows = lax.broadcasted_iota(jnp.int32, (ROWS, CH), 0)
    return jnp.where(rows < jnp.broadcast_to(meta_ref[0:1], (ROWS, CH)), 1.0, 0.0)


def sums_of(conv_out, meta_ref):
    kept = conv_out * live_rows(meta_ref)
    first = jnp.sum(kept, axis=0, keepdims=True)
    second = jnp.sum(kept * conv_out, axis=0, keepdims=True)
    return jnp.concatenate([first, second, meta_ref[0:1].astype(jnp.float32)], axis=1)


def write_sums(sums_ref, sums):
    for i in range(sums_ref.shape[0]):
        sums_ref[i] = sums


def total_of(stats_ref):
    total = stats_ref[0]
    for i in range(1, stats_ref.shape[0]):
        total = total + stats_ref[i]
    return total


def near_kernel(stats_ref, out_ref):
    write_sums(out_ref, total_of(stats_ref))


def scale_of(sums, gain, shift):
    total = sums[:, 2 * CH :]
    average = sums[:, :CH] / total
    variance = sums[:, CH : 2 * CH] / total - average * average
    scale = lax.rsqrt(variance + EPSILON) * gain
    return average, scale, shift


def affine(values, average, scale, shift):
    return (values - average) * scale + shift


def finish_kernel(meta_ref, second_ref, rows_ref, stats_ref, gain_ref, shift_ref, out_ref):
    stats = total_of(stats_ref)
    norm = scale_of(stats, gain_ref[...], shift_ref[...])
    summed = affine(second_ref[...], *norm) + rows_ref[...].astype(jnp.float32)
    out_ref[...] = (live_rows(meta_ref) * jnp.maximum(summed, 0.0)).astype(jnp.bfloat16)


def call(kernel, outs, scratch, limit, *args, hbm=False):
    vmem = pl.BlockSpec(memory_space=pltpu.VMEM)
    if hbm:
        args = [pltpu.with_memory_space_constraint(a, pltpu.HBM) for a in args]
    return pl.pallas_call(
        kernel,
        out_shape=outs,
        in_specs=[pl.BlockSpec(memory_space=pltpu.HBM) if hbm else vmem] * len(args),
        out_specs=jax.tree.map(lambda _: vmem, outs),
        scratch_shapes=scratch,
        compiler_params=pltpu.CompilerParams(vmem_limit_bytes=limit << 20),
    )(*args)


def conv_scratch():
    padded = -(-SIDES * SLOTS // CH) * CH
    return [
        pltpu.VMEM((SIDES * SLOTS, ROWS), jnp.bfloat16),
        pltpu.VMEM((ROWS, padded), jnp.bfloat16),
        pltpu.VMEM((padded, 2 * CH), jnp.bfloat16),
    ]


def slab_neighbours(to_low, to_high):
    count = lax.axis_size(SLAB)
    even = lax.axis_index("slab_2") == 0
    across = [(i, i + 1) for i in range(1, count - 1, 2)] + [(i + 1, i) for i in range(1, count - 1, 2)]
    far = lax.ppermute(jnp.where(even, to_low, to_high), SLAB, across)
    both = lax.all_gather(jnp.where(even, to_high, to_low), "slab_2")
    return jnp.where(even, far, both[0]), jnp.where(even, both[1], far)


def tile_neighbours(to_low, to_high):
    count = lax.axis_size("tile")
    forward = [(i, i + 1) for i in range(count - 1)]
    backward = [(j, i) for i, j in forward]
    low = lax.ppermute(to_high, "tile", forward)
    high = lax.ppermute(to_low, "tile", backward)
    return low, high


def reduce_all(sums):
    near = lax.all_to_all(sums, ("slab_1", "slab_2"), 0, 0)
    far = lax.axis_size(("slab_0", "tile"))
    block = call(near_kernel, jax.ShapeDtypeStruct((far, 1, 3 * CH), jnp.float32), [], 4, near)
    return lax.all_to_all(block, ("slab_0", "tile"), 0, 0)


def per_device(
    features, counts, rulebook, face_rows, conv_one, gain_one, shift_one, conv_two, gain_two, shift_two
):
    del counts
    f32, bf16, i32 = jnp.float32, jnp.bfloat16, jnp.int32
    shaped = jax.ShapeDtypeStruct
    ext, message, big = shaped((EXT, CH), f32), shaped((2 * SIDE_ROWS, CH), f32), shaped((ROWS, CH), f32)
    small = shaped((8, 1, 3 * CH), f32)
    params = (conv_two, gain_one[None], shift_one[None], gain_two[None], shift_two[None])
    outs = (
        ext, message, message,
        shaped((32, ROWS), i32), shaped((ROWS, CH), i32), shaped((CH, ROWS), bf16), shaped((8, CH), i32),
        shaped((ROWS, CH), bf16), shaped((4, FACE), i32), *(shaped(p.shape, p.dtype) for p in params),
    )
    scratch = [
        pltpu.VMEM((TAPS, 1, ROWS), i32), pltpu.VMEM((TAPS, CH, CH), bf16), pltpu.VMEM((32, ROWS), i32),
        *conv_scratch(), pltpu.SemaphoreType.DMA((9,)),
    ]
    taps = rulebook.reshape(TAPS, 1, ROWS)
    first, up, down, *plan, meta, rows, faces, weight_two, gain_one, shift_one, gain_two, shift_two = call(
        spread_kernel, outs, scratch, 24, taps, features[0, 0], conv_one, face_rows[0, 0], *params, hbm=True
    )
    total = SIDES * SLOTS
    outs = (shaped((total, ROWS), bf16), shaped((total, CH), i32))
    received = tile_neighbours(down, up)
    source = call(source_kernel, outs, conv_scratch()[:1], 8, plan[0], plan[2])
    first, left, right = call(tile_kernel, (ext, message, message), [], 8, first, *received, faces)
    received = slab_neighbours(left, right)
    first, sums = call(slab_kernel, (ext, small), [], 8, meta, first, *received, faces)
    stats = reduce_all(sums)
    second, sums = call(
        gather_kernel, (big, small), [pltpu.VMEM((ROWS, 2 * CH), bf16), *conv_scratch()], 24,
        meta, first, *plan, *source, weight_two, stats, gain_one, shift_one,
    )
    stats = reduce_all(sums)
    out = call(
        finish_kernel, shaped((ROWS, CH), bf16), [], 4, meta, second, rows, stats, gain_two, shift_two
    )
    return out[None, None]


def solution(mesh):
    tiles = mesh.shape["tile"]
    torus = Mesh(
        mesh.devices.reshape(-1, 4, 2, tiles), ("slab_0", "slab_1", "slab_2", "tile")
    )
    split = P(SLAB, "tile", None, None)
    in_specs = (split, P(SLAB, "tile"), split, split, P(), P(), P(), P(), P(), P())
    return jax.shard_map(
        per_device, mesh=torus, in_specs=in_specs, out_specs=split, check_vma=False
    )
```

profile of v0, /device:TPU:1, one launch (start us, length us, event | category | flops | bytes accessed | tf_op | source)
XLA Modules:
  0.0 86.6 jit_solution(16981810774798120678)
XLA Ops:
  0.0 3.3 %shard_map.91 = (f32[832,128]{1,0:T(8,128)S(1)}, f32[160,128]{1,0:T(8,128)S(1)}, f32[160,128]{1,0:T(8,128)S(1)}, s32[32,512]{1,0:T(8,128)S(1)}, s32[512,128]{1,0...) custom-call(s32[27,1,512]{2,1,0:T(1,128)} %bitcast.9, ...), custom_call_target="tpu_custom_call" | custom-call | tf_op jit(solution)/shard_map/pallas_call | solution.py:309
  3.3 4.0 %collective-permute-start = (f32[160,128]{1,0:T(8,128)S(1)}, f32[160,128]{1,0:T(8,128)S(1)}, u32[]{:S(2)}, u32[]{:S(2)}) collective-permute-start(f32[160,128]{1,0:T(8,128)S(1)} %get-tuple-element.30), channel_id=1, source_target_pairs={{0,1},{1,2},{2,3},{3,4},{4,5},{5,6},{6,7},{8,9},{9,10},{10,11},{11... | collective-permute-start | bytes 245768 | tf_op jit(solution)/shard_map/ppermute | solution.py:341
  7.4 1.3 %collective-permute-start.1 = (f32[160,128]{1,0:T(8,128)S(1)}, f32[160,128]{1,0:T(8,128)S(1)}, u32[]{:S(2)}, u32[]{:S(2)}) collective-permute-start(f32[160,128]{1,0:T(8,128)S(1)} %get-tuple-element.31), channel_id=1, source_target_pairs={{1,0},{2,1},{3,2},{4,3},{5,4},{6,5},{7,6},{9,8},{10,9},{11,10},{12... | collective-permute-start | bytes 245768 | tf_op jit(solution)/shard_map/ppermute | solution.py:342
  8.7 0.2 collective-permute-done.low_ref
  8.8 3.7 %collective-permute-done.1.high_ref = f32[160,128]{1,0:T(8,128)S(1)} collective-permute-done((f32[160,128]{1,0:T(8,128)S(1)}, f32[160,128]{1,0:T(8,128)S(1)}, u32[]{:S(2)}, u32[]{:S(2)}) %collective-permute-start.1) | collective-permute-done | bytes 81952 | tf_op jit(solution)/shard_map/ppermute | solution.py:342
  12.5 0.6 shard_map.92
  13.1 5.1 %collective-permute-start.2 = (f32[160,128]{1,0:T(8,128)S(1)}, f32[160,128]{1,0:T(8,128)S(1)}, u32[]{:S(2)}, u32[]{:S(2)}) collective-permute-start(f32[160,128]{1,0:T(8,128)S(1)} %get-tuple-element.54), channel_id=1, source_target_pairs={{8,16},{24,32},{40,48},{56,64},{72,80},{88,96},{104,112},{120,128}... | collective-permute-start | bytes 245768 | tf_op jit(solution)/shard_map/ppermute | solution.py:332
  18.2 2.4 %all-gather = f32[320,128]{1,0:T(8,128)S(1)} all-gather(f32[160,128]{1,0:T(8,128)S(1)} %get-tuple-element.53), channel_id=2, replica_groups=mesh['slab_0'=8,'slab_1'=4,'slab_2'=2,'tile'=8] {'slab_2'}, dimensions={0}, use_global_device_ids=true | all-gather | bytes 245760 | tf_op jit(solution)/shard_map/all_gather | solution.py:333
  20.6 0.0 collective-permute-done.2
  20.6 0.3 shard_map.93
  21.0 9.1 %all_to_all.20.stats_ref = f32[8,1,384]{2,1,0:T(1,128)S(1)} all-to-all(f32[8,1,384]{2,1,0:T(1,128)S(1)} %get-tuple-element.43), channel_id=1, replica_groups=mesh['slab_0'=8,'slab_1'=4,'slab_2'=2,'tile'=8] {'slab_1','slab_2'}, dimensions={0} | all-to-all | bytes 24576 | tf_op jit(solution)/shard_map/all_to_all | solution.py:347
  30.1 0.7 shard_map.95
  30.7 18.0 %all-to-all-start.1 = ((f32[64,1,384]{2,1,0:T(1,128)}), f32[64,1,384]{2,1,0:T(1,128)S(1)}, u32[]{:S(2)}, u32[]{:S(2)}) async-start(f32[64,1,384]{2,1,0:T(1,128)} %shard_map.95), calls=%async_computation.1 | async-start | bytes 196608 | tf_op jit(solution)/shard_map/all_to_all | solution.py:350
  48.8 0.5 shard_map.94
  49.3 10.9 %all-to-all-done.1.stats_ref = f32[64,1,384]{2,1,0:T(1,128)S(1)} async-done(((f32[64,1,384]{2,1,0:T(1,128)}), f32[64,1,384]{2,1,0:T(1,128)S(1)}, u32[]{:S(2)}, u32[]{:S(2)}) %all-to-all-start.1) | async-done | bytes 98336 | tf_op jit(solution)/shard_map/all_to_all | solution.py:350
  60.2 1.5 %shard_map.96 = (f32[512,128]{1,0:T(8,128)S(1)}, f32[8,1,384]{2,1,0:T(1,128)S(1)}) custom-call(s32[8,128]{1,0:T(8,128)S(1)} %get-tuple-element.28.meta_ref, f32[832,128]{1,0:T(8,128)S(1)} %get-tuple-element.36.first_ref, s32[32,512]{1,0:T(8,128)S(1)} %get-tuple-element.37.rank_ref, s32[512,128]{1,0:T(8,128)S(1)} %get-tuple-element.38.rank_t_ref, ...), custom_call_target="tpu_custom_call" | custom-call | tf_op jit(solution)/shard_map/pallas_call | solution.py:309
  61.7 9.0 %all_to_all.21.stats_ref = f32[8,1,384]{2,1,0:T(1,128)S(1)} all-to-all(f32[8,1,384]{2,1,0:T(1,128)S(1)} %get-tuple-element.48), channel_id=1, replica_groups=mesh['slab_0'=8,'slab_1'=4,'slab_2'=2,'tile'=8] {'slab_1','slab_2'}, dimensions={0} | all-to-all | bytes 24576 | tf_op jit(solution)/shard_map/all_to_all | solution.py:347
  70.7 15.1 %all_to_all.22.stats_ref = f32[64,1,384]{2,1,0:T(1,128)S(1)} all-to-all(f32[64,1,384]{2,1,0:T(1,128)S(1)} %shard_map.97), channel_id=1, replica_groups=mesh['slab_0'=8,'slab_1'=4,'slab_2'=2,'tile'=8] {'slab_0','tile'}, dimensions={0} | all-to-all | bytes 196608 | tf_op jit(solution)/shard_map/all_to_all | solution.py:350
  85.8 0.8 shard_map.98
  (3 shorter events, 0.1 us)
Async XLA Ops:
  3.3 5.5 %collective-permute-start = (f32[160,128]{1,0:T(8,128)S(1)}, f32[160,128]{1,0:T(8,128)S(1)}, u32[]{:S(2)}, u32[]{:S(2)}) collective-permute-start(f32[160,128]{1,0:T(8,128)S(1)} %get-tuple-element.30), channel_id=1, source_target_pairs={{0,1},{1,2},{2,3},{3,4},{4,5},{5,6},{6,7},{8,9},{9,10},{10,11},{11... | collective-permute-start | bytes 245768 | tf_op jit(solution)/shard_map/ppermute | solution.py:341
  7.4 5.2 %collective-permute-start.1 = (f32[160,128]{1,0:T(8,128)S(1)}, f32[160,128]{1,0:T(8,128)S(1)}, u32[]{:S(2)}, u32[]{:S(2)}) collective-permute-start(f32[160,128]{1,0:T(8,128)S(1)} %get-tuple-element.31), channel_id=1, source_target_pairs={{1,0},{2,1},{3,2},{4,3},{5,4},{6,5},{7,6},{9,8},{10,9},{11,10},{12... | collective-permute-start | bytes 245768 | tf_op jit(solution)/shard_map/ppermute | solution.py:342
  13.1 7.5 %collective-permute-start.2 = (f32[160,128]{1,0:T(8,128)S(1)}, f32[160,128]{1,0:T(8,128)S(1)}, u32[]{:S(2)}, u32[]{:S(2)}) collective-permute-start(f32[160,128]{1,0:T(8,128)S(1)} %get-tuple-element.54), channel_id=1, source_target_pairs={{8,16},{24,32},{40,48},{56,64},{72,80},{88,96},{104,112},{120,128}... | collective-permute-start | bytes 245768 | tf_op jit(solution)/shard_map/ppermute | solution.py:332
  30.7 29.5 %all-to-all-start.1 = ((f32[64,1,384]{2,1,0:T(1,128)}), f32[64,1,384]{2,1,0:T(1,128)S(1)}, u32[]{:S(2)}, u32[]{:S(2)}) async-start(f32[64,1,384]{2,1,0:T(1,128)} %shard_map.95), calls=%async_computation.1 | async-start | bytes 196608 | tf_op jit(solution)/shard_map/all_to_all | solution.py:350
where the time goes:
time: 87 us; the launch traced here: 86.6 us
  blocking collectives  35.6 us (41%)
  starting transfers between devices  28.5 us (33%)
  waiting for transfers between devices  14.8 us (17%)
  Pallas kernels  7.64 us (9%)
    all_to_all x2, blocking collectives, reduce_all(): near = lax.all_to_all(sums, ('slab_1', 'slab_2'), 0, 0)  18.1 us
    all_to_all x1, starting transfers between devices, reduce_all(): return lax.all_to_all(block, ('slab_0', 'tile'), 0, 0)  18 us
    all_to_all x1, blocking collectives, reduce_all(): return lax.all_to_all(block, ('slab_0', 'tile'), 0, 0)  15.1 us
    all_to_all x1, waiting for transfers between devices, reduce_all(): return lax.all_to_all(block, ('slab_0', 'tile'), 0, 0)  10.9 us
    pallas_call x8, Pallas kernels, call(): pl.pallas_call(kernel, out_shape=outs, in_specs=[pl.BlockSpec(memory_spac...  7.64 us
    ppermute x1, starting transfers between devices, slab_neighbours(): far = lax.ppermute(jnp.where(even, to_low, to_high), SLAB, across)  5.1 us
    ppermute x1, starting transfers between devices, tile_neighbours(): low = lax.ppermute(to_high, 'tile', forward)  4.02 us
    ppermute x1, waiting for transfers between devices, tile_neighbours(): high = lax.ppermute(to_low, 'tile', backward)  3.72 us
  transfers between devices with their start and end apart: 4, of which 3 were waited for; matrix products, arithmetic and copies ran while one was open for 0% of the time, Pallas kernels for 1%

commit v1 on v0

--- a/solution.py
+++ b/solution.py
@@ -62,7 +62,7 @@
 
 
 def put(selector, values):
-    return dot(jnp.concatenate([selector] * 3, axis=1), jnp.concatenate(thirds(values), axis=0))
+    return dot(selector, jnp.concatenate(values, axis=0).astype(jnp.bfloat16))
 
 
 def plan_pairs(rb_ref, work_ref, rank_ref, rank_t_ref, digits_ref):
@@ -165,42 +165,41 @@
         copy.wait()
     picked = pick(face_hot(faces_ref, 2), out_ref[:ROWS])
     for ref, own, at, far in ((down_ref, picked[:FACE], 0, QH), (up_ref, picked[FACE:], FACE - COLUMN, QL)):
-        ref[:COLUMN] = out_ref[A + at : A + at + COLUMN]
-        ref[COLUMN : COLUMN + FACE] = own
-        ref[COLUMN + FACE : SIDE_ROWS] = out_ref[B + at : B + at + COLUMN]
-        ref[SIDE_ROWS:] = out_ref[far : far + SIDE_ROWS]
+        pieces = [out_ref[A + at : A + at + COLUMN], own, out_ref[B + at : B + at + COLUMN]]
+        ref[...] = jnp.concatenate([*pieces, out_ref[far : far + SIDE_ROWS]], axis=0).astype(jnp.bfloat16)
 
 
 def tile_kernel(sums_ref, low_ref, high_ref, faces_ref, out_ref, left_ref, right_ref):
     out_ref[...] = sums_ref[...]
     first, last = SIDE_ROWS + COLUMN, SIDE_ROWS + COLUMN + FACE
-    out_ref[QH:QL] += low_ref[:SIDE_ROWS]
-    out_ref[QL : QL + SIDE_ROWS] += high_ref[:SIDE_ROWS]
-    for ref, at in ((low_ref, 0), (high_ref, FACE - COLUMN)):
-        out_ref[A + at : A + at + COLUMN] += ref[SIDE_ROWS:first]
-        out_ref[B + at : B + at + COLUMN] += ref[last:]
-    out_ref[:ROWS] += put(face_hot(faces_ref, 2), jnp.concatenate([low_ref[first:last], high_ref[first:last]], axis=0))
+    low, high = low_ref[...].astype(jnp.float32), high_ref[...].astype(jnp.float32)
+    out_ref[QH:QL] += low[:SIDE_ROWS]
+    out_ref[QL : QL + SIDE_ROWS] += high[:SIDE_ROWS]
+    for sent, at in ((low, 0), (high, FACE - COLUMN)):
+        out_ref[A + at : A + at + COLUMN] += sent[SIDE_ROWS:first]
+        out_ref[B + at : B + at + COLUMN] += sent[last:]
+    out_ref[:ROWS] += put(face_hot(faces_ref, 2), [low[first:last], high[first:last]])
     picked = pick(face_hot(faces_ref, 0), out_ref[:ROWS])
     for ref, own, own_at, far, far_at in (
         (left_ref, picked[:FACE], COLUMN, A, 0),
         (right_ref, picked[FACE:], FACE, B, FACE + COLUMN),
     ):
-        ref[:FACE] = own
-        ref[SIDE_ROWS : SIDE_ROWS + FACE] = out_ref[far : far + FACE]
-        for start, at in ((0, own_at), (SIDE_ROWS, far_at)):
-            ref[start + FACE : start + FACE + COLUMN] = out_ref[QH + at : QH + at + COLUMN]
-            ref[start + FACE + COLUMN : start + SIDE_ROWS] = out_ref[QL + at : QL + at + COLUMN]
+        pieces = []
+        for face, at in ((own, own_at), (out_ref[far : far + FACE], far_at)):
+            pieces += [face, out_ref[QH + at : QH + at + COLUMN], out_ref[QL + at : QL + at + COLUMN]]
+        ref[...] = jnp.concatenate(pieces, axis=0).astype(jnp.bfloat16)
 
 
 def slab_kernel(meta_ref, sums_ref, low_ref, high_ref, faces_ref, out_ref, stats_ref):
     out_ref[...] = sums_ref[...]
-    for ref, far, far_at, own_at in ((low_ref, A, 0, COLUMN), (high_ref, B, FACE + COLUMN, FACE)):
-        out_ref[far : far + FACE] += ref[:FACE]
+    low, high = low_ref[...].astype(jnp.float32), high_ref[...].astype(jnp.float32)
+    for sent, far, far_at, own_at in ((low, A, 0, COLUMN), (high, B, FACE + COLUMN, FACE)):
+        out_ref[far : far + FACE] += sent[:FACE]
         for start, at in ((0, far_at), (SIDE_ROWS, own_at)):
-            out_ref[QH + at : QH + at + COLUMN] += ref[start + FACE : start + FACE + COLUMN]
-            out_ref[QL + at : QL + at + COLUMN] += ref[start + FACE + COLUMN : start + SIDE_ROWS]
+            out_ref[QH + at : QH + at + COLUMN] += sent[start + FACE : start + FACE + COLUMN]
+            out_ref[QL + at : QL + at + COLUMN] += sent[start + FACE + COLUMN : start + SIDE_ROWS]
     own = slice(SIDE_ROWS, SIDE_ROWS + FACE)
-    total = out_ref[:ROWS] + put(face_hot(faces_ref, 0), jnp.concatenate([low_ref[own], high_ref[own]], axis=0))
+    total = out_ref[:ROWS] + put(face_hot(faces_ref, 0), [low[own], high[own]])
     out_ref[:ROWS] = total
     write_sums(stats_ref, sums_of(total, meta_ref))
 
@@ -356,7 +355,7 @@
     del counts
     f32, bf16, i32 = jnp.float32, jnp.bfloat16, jnp.int32
     shaped = jax.ShapeDtypeStruct
-    ext, message, big = shaped((EXT, CH), f32), shaped((2 * SIDE_ROWS, CH), f32), shaped((ROWS, CH), f32)
+    ext, message, big = shaped((EXT, CH), f32), shaped((2 * SIDE_ROWS, CH), bf16), shaped((ROWS, CH), f32)
     small = shaped((8, 1, 3 * CH), f32)
     params = (conv_two, gain_one[None], shift_one[None], gain_two[None], shift_two[None])
     outs = (

time: 87 us -> 85.9 us (0.987)
  transfers between devices with their start and end apart: 4 -> 4, of which waited for: 3 -> 2; matrix products, arithmetic and copies ran while one was open for 0% -> 0% of each run, Pallas kernels for 1% -> 1%
where the time goes in v1:
time: 85.9 us; the launch traced here: 85.6 us
  blocking collectives  35.4 us (41%)
  starting transfers between devices  28.2 us (33%)
  waiting for transfers between devices  14.4 us (17%)
  Pallas kernels  7.48 us (9%)
    all_to_all x2, blocking collectives, reduce_all(): near = lax.all_to_all(sums, ('slab_1', 'slab_2'), 0, 0)  18 us
    all_to_all x1, starting transfers between devices, reduce_all(): return lax.all_to_all(block, ('slab_0', 'tile'), 0, 0)  17.8 us
    all_to_all x1, blocking collectives, reduce_all(): return lax.all_to_all(block, ('slab_0', 'tile'), 0, 0)  15.1 us
    all_to_all x1, waiting for transfers between devices, reduce_all(): return lax.all_to_all(block, ('slab_0', 'tile'), 0, 0)  10.9 us
    pallas_call x8, Pallas kernels, call(): pl.pallas_call(kernel, out_shape=outs, in_specs=[pl.BlockSpec(memory_spac...  7.48 us
    ppermute x1, starting transfers between devices, slab_neighbours(): far = lax.ppermute(jnp.where(even, to_low, to_high), SLAB, across)  5.11 us
    ppermute x1, starting transfers between devices, tile_neighbours(): low = lax.ppermute(to_high, 'tile', forward)  4.02 us
    ppermute x1, waiting for transfers between devices, tile_neighbours(): high = lax.ppermute(to_low, 'tile', backward)  3.43 us
  transfers between devices with their start and end apart: 4, of which 2 were waited for; matrix products, arithmetic and copies ran while one was open for 0% of the time, Pallas kernels for 1%

profile of v1, /device:TPU:1, one launch (start us, length us, event | category | flops | bytes accessed | tf_op | source)
XLA Modules:
  0.0 85.6 jit_solution(1365671925451802900)
XLA Ops:
  0.0 3.3 %shard_map.91 = (f32[832,128]{1,0:T(8,128)S(1)}, bf16[160,128]{1,0:T(8,128)(2,1)S(1)}, bf16[160,128]{1,0:T(8,128)(2,1)S(1)}, s32[32,512]{1,0:T(8,128)S(1)}, s32[...) custom-call(s32[27,1,512]{2,1,0:T(1,128)} %bitcast.9, ...), custom_call_target="tpu_custom_call" | custom-call | tf_op jit(solution)/shard_map/pallas_call | solution.py:308
  3.3 4.0 %collective-permute-start = (bf16[160,128]{1,0:T(8,128)(2,1)S(1)}, bf16[160,128]{1,0:T(8,128)(2,1)S(1)}, u32[]{:S(2)}, u32[]{:S(2)}) collective-permute-start(bf16[160,128]{1,0:T(8,128)(2,1)S(1)} %get-tuple-element.30), channel_id=1, source_target_pairs={{0,1},{1,2},{2,3},{3,4},{4,5},{5,6},{6,7},{8,9},{9,10},{10,11},{11... | collective-permute-start | bytes 122888 | tf_op jit(solution)/shard_map/ppermute | solution.py:340
  7.4 1.3 %collective-permute-start.1 = (bf16[160,128]{1,0:T(8,128)(2,1)S(1)}, bf16[160,128]{1,0:T(8,128)(2,1)S(1)}, u32[]{:S(2)}, u32[]{:S(2)}) collective-permute-start(bf16[160,128]{1,0:T(8,128)(2,1)S(1)} %get-tuple-element.31), channel_id=1, source_target_pairs={{1,0},{2,1},{3,2},{4,3},{5,4},{6,5},{7,6},{9,8},{10,9},{11,10},{12... | collective-permute-start | bytes 122888 | tf_op jit(solution)/shard_map/ppermute | solution.py:341
  8.7 0.0 collective-permute-done.low_ref
  8.7 3.4 %collective-permute-done.1.high_ref = bf16[160,128]{1,0:T(8,128)(2,1)S(1)} collective-permute-done((bf16[160,128]{1,0:T(8,128)(2,1)S(1)}, bf16[160,128]{1,0:T(8,128)(2,1)S(1)}, u32[]{:S(2)}, u32[]{:S(2)}) %collective-permute-start.1) | collective-permute-done | bytes 40992 | tf_op jit(solution)/shard_map/ppermute | solution.py:341
  12.1 0.5 shard_map.92
  12.6 5.1 %collective-permute-start.2 = (bf16[160,128]{1,0:T(8,128)(2,1)S(1)}, bf16[160,128]{1,0:T(8,128)(2,1)S(1)}, u32[]{:S(2)}, u32[]{:S(2)}) collective-permute-start(bf16[160,128]{1,0:T(8,128)(2,1)S(1)} %get-tuple-element.54), channel_id=1, source_target_pairs={{8,16},{24,32},{40,48},{56,64},{72,80},{88,96},{104,112},{120,128}... | collective-permute-start | bytes 122888 | tf_op jit(solution)/shard_map/ppermute | solution.py:331
  17.7 2.3 %all-gather = bf16[320,128]{1,0:T(8,128)(2,1)S(1)} all-gather(bf16[160,128]{1,0:T(8,128)(2,1)S(1)} %get-tuple-element.53), channel_id=2, replica_groups=mesh['slab_0'=8,'slab_1'=4,'slab_2'=2,'tile'=8] {'slab_2'}, dimensions={0}, use_global_device_ids=true | all-gather | bytes 122880 | tf_op jit(solution)/shard_map/all_gather | solution.py:332
  20.0 0.0 collective-permute-done.2
  20.0 0.3 shard_map.93
  20.3 9.0 %all_to_all.20.stats_ref = f32[8,1,384]{2,1,0:T(1,128)S(1)} all-to-all(f32[8,1,384]{2,1,0:T(1,128)S(1)} %get-tuple-element.43), channel_id=1, replica_groups=mesh['slab_0'=8,'slab_1'=4,'slab_2'=2,'tile'=8] {'slab_1','slab_2'}, dimensions={0} | all-to-all | bytes 24576 | tf_op jit(solution)/shard_map/all_to_all | solution.py:346
  29.3 0.7 shard_map.95
  29.9 17.8 %all-to-all-start.1 = ((f32[64,1,384]{2,1,0:T(1,128)}), f32[64,1,384]{2,1,0:T(1,128)S(1)}, u32[]{:S(2)}, u32[]{:S(2)}) async-start(f32[64,1,384]{2,1,0:T(1,128)} %shard_map.95), calls=%async_computation.1 | async-start | bytes 196608 | tf_op jit(solution)/shard_map/all_to_all | solution.py:349
  47.8 0.5 shard_map.94
  48.2 10.9 %all-to-all-done.1.stats_ref = f32[64,1,384]{2,1,0:T(1,128)S(1)} async-done(((f32[64,1,384]{2,1,0:T(1,128)}), f32[64,1,384]{2,1,0:T(1,128)S(1)}, u32[]{:S(2)}, u32[]{:S(2)}) %all-to-all-start.1) | async-done | bytes 98336 | tf_op jit(solution)/shard_map/all_to_all | solution.py:349
  59.2 1.5 %shard_map.96 = (f32[512,128]{1,0:T(8,128)S(1)}, f32[8,1,384]{2,1,0:T(1,128)S(1)}) custom-call(s32[8,128]{1,0:T(8,128)S(1)} %get-tuple-element.28.meta_ref, f32[832,128]{1,0:T(8,128)S(1)} %get-tuple-element.36.first_ref, s32[32,512]{1,0:T(8,128)S(1)} %get-tuple-element.37.rank_ref, s32[512,128]{1,0:T(8,128)S(1)} %get-tuple-element.38.rank_t_ref, ...), custom_call_target="tpu_custom_call" | custom-call | tf_op jit(solution)/shard_map/pallas_call | solution.py:308
  60.6 9.0 %all_to_all.21.stats_ref = f32[8,1,384]{2,1,0:T(1,128)S(1)} all-to-all(f32[8,1,384]{2,1,0:T(1,128)S(1)} %get-tuple-element.48), channel_id=1, replica_groups=mesh['slab_0'=8,'slab_1'=4,'slab_2'=2,'tile'=8] {'slab_1','slab_2'}, dimensions={0} | all-to-all | bytes 24576 | tf_op jit(solution)/shard_map/all_to_all | solution.py:346
  69.7 15.1 %all_to_all.22.stats_ref = f32[64,1,384]{2,1,0:T(1,128)S(1)} all-to-all(f32[64,1,384]{2,1,0:T(1,128)S(1)} %shard_map.97), channel_id=1, replica_groups=mesh['slab_0'=8,'slab_1'=4,'slab_2'=2,'tile'=8] {'slab_0','tile'}, dimensions={0} | all-to-all | bytes 196608 | tf_op jit(solution)/shard_map/all_to_all | solution.py:349
  84.8 0.8 shard_map.98
  (3 shorter events, 0.1 us)
Async XLA Ops:
  3.3 5.3 %collective-permute-start = (bf16[160,128]{1,0:T(8,128)(2,1)S(1)}, bf16[160,128]{1,0:T(8,128)(2,1)S(1)}, u32[]{:S(2)}, u32[]{:S(2)}) collective-permute-start(bf16[160,128]{1,0:T(8,128)(2,1)S(1)} %get-tuple-element.30), channel_id=1, source_target_pairs={{0,1},{1,2},{2,3},{3,4},{4,5},{5,6},{6,7},{8,9},{9,10},{10,11},{11... | collective-permute-start | bytes 122888 | tf_op jit(solution)/shard_map/ppermute | solution.py:340
  7.4 4.7 %collective-permute-start.1 = (bf16[160,128]{1,0:T(8,128)(2,1)S(1)}, bf16[160,128]{1,0:T(8,128)(2,1)S(1)}, u32[]{:S(2)}, u32[]{:S(2)}) collective-permute-start(bf16[160,128]{1,0:T(8,128)(2,1)S(1)} %get-tuple-element.31), channel_id=1, source_target_pairs={{1,0},{2,1},{3,2},{4,3},{5,4},{6,5},{7,6},{9,8},{10,9},{11,10},{12... | collective-permute-start | bytes 122888 | tf_op jit(solution)/shard_map/ppermute | solution.py:341
  12.6 7.4 %collective-permute-start.2 = (bf16[160,128]{1,0:T(8,128)(2,1)S(1)}, bf16[160,128]{1,0:T(8,128)(2,1)S(1)}, u32[]{:S(2)}, u32[]{:S(2)}) collective-permute-start(bf16[160,128]{1,0:T(8,128)(2,1)S(1)} %get-tuple-element.54), channel_id=1, source_target_pairs={{8,16},{24,32},{40,48},{56,64},{72,80},{88,96},{104,112},{120,128}... | collective-permute-start | bytes 122888 | tf_op jit(solution)/shard_map/ppermute | solution.py:331
  29.9 29.2 %all-to-all-start.1 = ((f32[64,1,384]{2,1,0:T(1,128)}), f32[64,1,384]{2,1,0:T(1,128)S(1)}, u32[]{:S(2)}, u32[]{:S(2)}) async-start(f32[64,1,384]{2,1,0:T(1,128)} %shard_map.95), calls=%async_computation.1 | async-start | bytes 196608 | tf_op jit(solution)/shard_map/all_to_all | solution.py:349

commit v2 on v1

--- a/solution.py
+++ b/solution.py
@@ -43,22 +43,14 @@
     return copies
 
 
-def thirds(values):
-    high = values.astype(jnp.bfloat16)
-    rest = values - high.astype(jnp.float32)
-    mid = rest.astype(jnp.bfloat16)
-    return high, mid, (rest - mid.astype(jnp.float32)).astype(jnp.bfloat16)
-
-
 def face_hot(faces_ref, k):
     return hot(jnp.concatenate([faces_ref[k : k + 1, :], faces_ref[k + 1 : k + 2, :]], axis=1), (ROWS, 2 * FACE), 0)
 
 
 def pick(selector, rows):
-    got = lax.dot_general(
-        selector, jnp.concatenate(thirds(rows), axis=1), (((0,), (0,)), ((), ())), preferred_element_type=jnp.float32
-    )
-    return got[:, :CH] + got[:, CH : 2 * CH] + got[:, 2 * CH :]
+    return lax.dot_general(
+        selector, rows.astype(jnp.bfloat16), (((0,), (0,)), ((), ())), preferred_element_type=jnp.float32
+    )
 
 
 def put(selector, values):
@@ -112,9 +104,11 @@
 
 
 def multiply_slots(picked, weight_ref, tap_of, part_ref):
-    parts = [
-        dot(picked[t * SLOTS : (t + 1) * SLOTS].astype(jnp.bfloat16), weight_ref[tap_of(t)]) for t in range(SIDES)
-    ]
+    parts = []
+    for t in range(0, SIDES, 2):
+        both = jnp.concatenate([weight_ref[tap_of(t)], weight_ref[tap_of(t + 1)]], axis=1)
+        got = dot(picked[t * SLOTS : (t + 2) * SLOTS].astype(jnp.bfloat16), both)
+        parts += [got[:SLOTS, :CH], got[SLOTS:, CH:]]
     part = jnp.concatenate(parts, axis=0)
     high = part.astype(jnp.bfloat16)
     part_ref[: SIDES * SLOTS, :CH] = high
@@ -272,10 +266,10 @@
 
 
 def total_of(stats_ref):
-    total = stats_ref[0]
-    for i in range(1, stats_ref.shape[0]):
-        total = total + stats_ref[i]
-    return total
+    parts = [stats_ref[i] for i in range(stats_ref.shape[0])]
+    while len(parts) > 1:
+        parts = [a + b for a, b in zip(parts[::2], parts[1::2], strict=True)]
+    return parts[0]
 
 
 def near_kernel(stats_ref, out_ref):

time: 85.9 us -> 85.6 us (level)
  no operation moved by 1% of the time
where the time goes in v2:
time: 85.6 us; the launch traced here: 85.3 us
  blocking collectives  35.4 us (41%)
  starting transfers between devices  28.2 us (33%)
  waiting for transfers between devices  14.4 us (17%)
  Pallas kernels  7.16 us (8%)
    all_to_all x2, blocking collectives, reduce_all(): near = lax.all_to_all(sums, ('slab_1', 'slab_2'), 0, 0)  18 us
    all_to_all x1, starting transfers between devices, reduce_all(): return lax.all_to_all(block, ('slab_0', 'tile'), 0, 0)  17.8 us
    all_to_all x1, blocking collectives, reduce_all(): return lax.all_to_all(block, ('slab_0', 'tile'), 0, 0)  15.1 us
    all_to_all x1, waiting for transfers between devices, reduce_all(): return lax.all_to_all(block, ('slab_0', 'tile'), 0, 0)  10.9 us
    pallas_call x8, Pallas kernels, call(): pl.pallas_call(kernel, out_shape=outs, in_specs=[pl.BlockSpec(memory_spac...  7.16 us
    ppermute x1, starting transfers between devices, slab_neighbours(): far = lax.ppermute(jnp.where(even, to_low, to_high), SLAB, across)  5.11 us
    ppermute x1, starting transfers between devices, tile_neighbours(): low = lax.ppermute(to_high, 'tile', forward)  4.02 us
    ppermute x1, waiting for transfers between devices, tile_neighbours(): high = lax.ppermute(to_low, 'tile', backward)  3.43 us
  transfers between devices with their start and end apart: 4, of which 2 were waited for; matrix products, arithmetic and copies ran while one was open for 0% of the time, Pallas kernels for 1%

profile of v2, /device:TPU:1, one launch (start us, length us, event | category | flops | bytes accessed | tf_op | source)
XLA Modules:
  0.0 85.3 jit_solution(2110374952123267860)
XLA Ops:
  0.0 3.2 %shard_map.91 = (f32[832,128]{1,0:T(8,128)S(1)}, bf16[160,128]{1,0:T(8,128)(2,1)S(1)}, bf16[160,128]{1,0:T(8,128)(2,1)S(1)}, s32[32,512]{1,0:T(8,128)S(1)}, s32[...) custom-call(s32[27,1,512]{2,1,0:T(1,128)} %bitcast.9, ...), custom_call_target="tpu_custom_call" | custom-call | tf_op jit(solution)/shard_map/pallas_call | solution.py:302
  3.2 4.0 %collective-permute-start = (bf16[160,128]{1,0:T(8,128)(2,1)S(1)}, bf16[160,128]{1,0:T(8,128)(2,1)S(1)}, u32[]{:S(2)}, u32[]{:S(2)}) collective-permute-start(bf16[160,128]{1,0:T(8,128)(2,1)S(1)} %get-tuple-element.30), channel_id=1, source_target_pairs={{0,1},{1,2},{2,3},{3,4},{4,5},{5,6},{6,7},{8,9},{9,10},{10,11},{11... | collective-permute-start | bytes 122888 | tf_op jit(solution)/shard_map/ppermute | solution.py:334
  7.3 1.3 %collective-permute-start.1 = (bf16[160,128]{1,0:T(8,128)(2,1)S(1)}, bf16[160,128]{1,0:T(8,128)(2,1)S(1)}, u32[]{:S(2)}, u32[]{:S(2)}) collective-permute-start(bf16[160,128]{1,0:T(8,128)(2,1)S(1)} %get-tuple-element.31), channel_id=1, source_target_pairs={{1,0},{2,1},{3,2},{4,3},{5,4},{6,5},{7,6},{9,8},{10,9},{11,10},{12... | collective-permute-start | bytes 122888 | tf_op jit(solution)/shard_map/ppermute | solution.py:335
  8.6 0.0 collective-permute-done.low_ref
  8.6 3.4 %collective-permute-done.1.high_ref = bf16[160,128]{1,0:T(8,128)(2,1)S(1)} collective-permute-done((bf16[160,128]{1,0:T(8,128)(2,1)S(1)}, bf16[160,128]{1,0:T(8,128)(2,1)S(1)}, u32[]{:S(2)}, u32[]{:S(2)}) %collective-permute-start.1) | collective-permute-done | bytes 40992 | tf_op jit(solution)/shard_map/ppermute | solution.py:335
  12.0 0.4 shard_map.92
  12.5 5.1 %collective-permute-start.2 = (bf16[160,128]{1,0:T(8,128)(2,1)S(1)}, bf16[160,128]{1,0:T(8,128)(2,1)S(1)}, u32[]{:S(2)}, u32[]{:S(2)}) collective-permute-start(bf16[160,128]{1,0:T(8,128)(2,1)S(1)} %get-tuple-element.54), channel_id=1, source_target_pairs={{8,16},{24,32},{40,48},{56,64},{72,80},{88,96},{104,112},{120,128}... | collective-permute-start | bytes 122888 | tf_op jit(solution)/shard_map/ppermute | solution.py:325
  17.6 2.3 %all-gather = bf16[320,128]{1,0:T(8,128)(2,1)S(1)} all-gather(bf16[160,128]{1,0:T(8,128)(2,1)S(1)} %get-tuple-element.53), channel_id=2, replica_groups=mesh['slab_0'=8,'slab_1'=4,'slab_2'=2,'tile'=8] {'slab_2'}, dimensions={0}, use_global_device_ids=true | all-gather | bytes 122880 | tf_op jit(solution)/shard_map/all_gather | solution.py:326
  19.9 0.0 collective-permute-done.2
  19.9 0.3 shard_map.93
  20.2 9.0 %all_to_all.20.stats_ref = f32[8,1,384]{2,1,0:T(1,128)S(1)} all-to-all(f32[8,1,384]{2,1,0:T(1,128)S(1)} %get-tuple-element.43), channel_id=1, replica_groups=mesh['slab_0'=8,'slab_1'=4,'slab_2'=2,'tile'=8] {'slab_1','slab_2'}, dimensions={0} | all-to-all | bytes 24576 | tf_op jit(solution)/shard_map/all_to_all | solution.py:340
  29.2 0.7 shard_map.95
  29.8 17.8 %all-to-all-start.1 = ((f32[64,1,384]{2,1,0:T(1,128)}), f32[64,1,384]{2,1,0:T(1,128)S(1)}, u32[]{:S(2)}, u32[]{:S(2)}) async-start(f32[64,1,384]{2,1,0:T(1,128)} %shard_map.95), calls=%async_computation.1 | async-start | bytes 196608 | tf_op jit(solution)/shard_map/all_to_all | solution.py:343
  47.6 0.5 shard_map.94
  48.1 10.9 %all-to-all-done.1.stats_ref = f32[64,1,384]{2,1,0:T(1,128)S(1)} async-done(((f32[64,1,384]{2,1,0:T(1,128)}), f32[64,1,384]{2,1,0:T(1,128)S(1)}, u32[]{:S(2)}, u32[]{:S(2)}) %all-to-all-start.1) | async-done | bytes 98336 | tf_op jit(solution)/shard_map/all_to_all | solution.py:343
  59.0 1.3 %shard_map.96 = (f32[512,128]{1,0:T(8,128)S(1)}, f32[8,1,384]{2,1,0:T(1,128)S(1)}) custom-call(s32[8,128]{1,0:T(8,128)S(1)} %get-tuple-element.28.meta_ref, f32[832,128]{1,0:T(8,128)S(1)} %get-tuple-element.36.first_ref, s32[32,512]{1,0:T(8,128)S(1)} %get-tuple-element.37.rank_ref, s32[512,128]{1,0:T(8,128)S(1)} %get-tuple-element.38.rank_t_ref, ...), custom_call_target="tpu_custom_call" | custom-call | tf_op jit(solution)/shard_map/pallas_call | solution.py:302
  60.3 9.0 %all_to_all.21.stats_ref = f32[8,1,384]{2,1,0:T(1,128)S(1)} all-to-all(f32[8,1,384]{2,1,0:T(1,128)S(1)} %get-tuple-element.48), channel_id=1, replica_groups=mesh['slab_0'=8,'slab_1'=4,'slab_2'=2,'tile'=8] {'slab_1','slab_2'}, dimensions={0} | all-to-all | bytes 24576 | tf_op jit(solution)/shard_map/all_to_all | solution.py:340
  69.4 15.1 %all_to_all.22.stats_ref = f32[64,1,384]{2,1,0:T(1,128)S(1)} all-to-all(f32[64,1,384]{2,1,0:T(1,128)S(1)} %shard_map.97), channel_id=1, replica_groups=mesh['slab_0'=8,'slab_1'=4,'slab_2'=2,'tile'=8] {'slab_0','tile'}, dimensions={0} | all-to-all | bytes 196608 | tf_op jit(solution)/shard_map/all_to_all | solution.py:343
  84.5 0.8 shard_map.98
  (3 shorter events, 0.0 us)
Async XLA Ops:
  3.2 5.3 %collective-permute-start = (bf16[160,128]{1,0:T(8,128)(2,1)S(1)}, bf16[160,128]{1,0:T(8,128)(2,1)S(1)}, u32[]{:S(2)}, u32[]{:S(2)}) collective-permute-start(bf16[160,128]{1,0:T(8,128)(2,1)S(1)} %get-tuple-element.30), channel_id=1, source_target_pairs={{0,1},{1,2},{2,3},{3,4},{4,5},{5,6},{6,7},{8,9},{9,10},{10,11},{11... | collective-permute-start | bytes 122888 | tf_op jit(solution)/shard_map/ppermute | solution.py:334
  7.3 4.7 %collective-permute-start.1 = (bf16[160,128]{1,0:T(8,128)(2,1)S(1)}, bf16[160,128]{1,0:T(8,128)(2,1)S(1)}, u32[]{:S(2)}, u32[]{:S(2)}) collective-permute-start(bf16[160,128]{1,0:T(8,128)(2,1)S(1)} %get-tuple-element.31), channel_id=1, source_target_pairs={{1,0},{2,1},{3,2},{4,3},{5,4},{6,5},{7,6},{9,8},{10,9},{11,10},{12... | collective-permute-start | bytes 122888 | tf_op jit(solution)/shard_map/ppermute | solution.py:335
  12.5 7.4 %collective-permute-start.2 = (bf16[160,128]{1,0:T(8,128)(2,1)S(1)}, bf16[160,128]{1,0:T(8,128)(2,1)S(1)}, u32[]{:S(2)}, u32[]{:S(2)}) collective-permute-start(bf16[160,128]{1,0:T(8,128)(2,1)S(1)} %get-tuple-element.54), channel_id=1, source_target_pairs={{8,16},{24,32},{40,48},{56,64},{72,80},{88,96},{104,112},{120,128}... | collective-permute-start | bytes 122888 | tf_op jit(solution)/shard_map/ppermute | solution.py:325
  29.8 29.2 %all-to-all-start.1 = ((f32[64,1,384]{2,1,0:T(1,128)}), f32[64,1,384]{2,1,0:T(1,128)S(1)}, u32[]{:S(2)}, u32[]{:S(2)}) async-start(f32[64,1,384]{2,1,0:T(1,128)} %shard_map.95), calls=%async_computation.1 | async-start | bytes 196608 | tf_op jit(solution)/shard_map/all_to_all | solution.py:343

commit v3 on v2

--- a/solution.py
+++ b/solution.py
@@ -329,11 +329,12 @@
 
 def tile_neighbours(to_low, to_high):
     count = lax.axis_size("tile")
-    forward = [(i, i + 1) for i in range(count - 1)]
-    backward = [(j, i) for i, j in forward]
-    low = lax.ppermute(to_high, "tile", forward)
-    high = lax.ppermute(to_low, "tile", backward)
-    return low, high
+    even = lax.axis_index("tile") % 2 == 0
+    inner = [(i, i ^ 1) for i in range(count)]
+    outer = [(i, i + 1) for i in range(1, count - 1, 2)] + [(i + 1, i) for i in range(1, count - 1, 2)]
+    one = lax.ppermute(jnp.where(even, to_high, to_low), "tile", inner)
+    two = lax.ppermute(jnp.where(even, to_low, to_high), "tile", outer)
+    return jnp.where(even, two, one), jnp.where(even, one, two)
 
 
 def reduce_all(sums):

time: 85.6 us -> 85.8 us (level)
  waiting for transfers between devices: 14.4 us -> 11.6 us
  starting transfers between devices: 28.2 us -> 30.5 us
    all_to_all x1, starting transfers between devices: 17.8 us -> 20.8 us  [reduce_all(): return lax.all_to_all(block, ('slab_0', 'tile'), 0, 0)]
    ppermute x2, waiting for transfers between devices: 3.43 us -> 0.7 us  [the longest x1 0.7 us: tile_neighbours(): one = lax.ppermute(jnp.where(even, to_high, to_low), 'tile', inner)]
    all_gather x1, blocking collectives: 2.32 us -> 4.52 us  [slab_neighbours(): both = lax.all_gather(jnp.where(even, to_high, to_low), 'slab_2')]
    all_to_all x2, blocking collectives: 18 us -> 16.4 us  [reduce_all(): near = lax.all_to_all(sums, ('slab_1', 'slab_2'), 0, 0)]
where the time goes in v3:
time: 85.8 us; the launch traced here: 85.4 us
  blocking collectives  36 us (42%)
  starting transfers between devices  30.5 us (36%)
  waiting for transfers between devices  11.6 us (14%)
  Pallas kernels  7.16 us (8%)
    all_to_all x1, starting transfers between devices, reduce_all(): return lax.all_to_all(block, ('slab_0', 'tile'), 0, 0)  20.8 us
    all_to_all x2, blocking collectives, reduce_all(): near = lax.all_to_all(sums, ('slab_1', 'slab_2'), 0, 0)  16.4 us
    all_to_all x1, blocking collectives, reduce_all(): return lax.all_to_all(block, ('slab_0', 'tile'), 0, 0)  15.1 us
    all_to_all x1, waiting for transfers between devices, reduce_all(): return lax.all_to_all(block, ('slab_0', 'tile'), 0, 0)  10.9 us
    pallas_call x8, Pallas kernels, call(): pl.pallas_call(kernel, out_shape=outs, in_specs=[pl.BlockSpec(memory_spac...  7.16 us
    ppermute x1, starting transfers between devices, slab_neighbours(): far = lax.ppermute(jnp.where(even, to_low, to_high), SLAB, across)  4.99 us
    all_gather x1, blocking collectives, slab_neighbours(): both = lax.all_gather(jnp.where(even, to_high, to_low), 'slab_2')  4.52 us
    ppermute x1, starting transfers between devices, tile_neighbours(): one = lax.ppermute(jnp.where(even, to_high, to_low), 'tile', inner)  4.02 us
  transfers between devices with their start and end apart: 4, of which 2 were waited for; matrix products, arithmetic and copies ran while one was open for 0% of the time, Pallas kernels for 1%

profile of v3, /device:TPU:1, one launch (start us, length us, event | category | flops | bytes accessed | tf_op | source)
XLA Modules:
  0.0 85.4 jit_solution(14451247852075231731)
XLA Ops:
  0.0 3.2 %shard_map.91 = (f32[832,128]{1,0:T(8,128)S(1)}, bf16[160,128]{1,0:T(8,128)(2,1)S(1)}, bf16[160,128]{1,0:T(8,128)(2,1)S(1)}, s32[32,512]{1,0:T(8,128)S(1)}, s32[...) custom-call(s32[27,1,512]{2,1,0:T(1,128)} %bitcast.9, ...), custom_call_target="tpu_custom_call" | custom-call | tf_op jit(solution)/shard_map/pallas_call | solution.py:302
  3.3 4.0 %collective-permute-start.1 = (bf16[160,128]{1,0:T(8,128)(2,1)S(1)}, bf16[160,128]{1,0:T(8,128)(2,1)S(1)}, u32[]{:S(2)}, u32[]{:S(2)}) collective-permute-start(bf16[160,128]{1,0:T(8,128)(2,1)S(1)} %get-tuple-element.57), channel_id=1, source_target_pairs={{0,1},{1,0},{2,3},{3,2},{4,5},{5,4},{6,7},{7,6},{8,9},{9,8},{10,11... | collective-permute-start | bytes 122888 | tf_op jit(solution)/shard_map/ppermute | solution.py:335
  7.3 0.7 collective-permute-start
  8.0 0.7 collective-permute-done.1
  8.7 0.0 collective-permute-done
  8.7 0.4 shard_map.92
  9.1 5.0 %collective-permute-start.2 = (bf16[160,128]{1,0:T(8,128)(2,1)S(1)}, bf16[160,128]{1,0:T(8,128)(2,1)S(1)}, u32[]{:S(2)}, u32[]{:S(2)}) collective-permute-start(bf16[160,128]{1,0:T(8,128)(2,1)S(1)} %get-tuple-element.54), channel_id=1, source_target_pairs={{8,16},{24,32},{40,48},{56,64},{72,80},{88,96},{104,112},{120,128}... | collective-permute-start | bytes 122888 | tf_op jit(solution)/shard_map/ppermute | solution.py:325
  14.1 4.5 %all-gather = bf16[320,128]{1,0:T(8,128)(2,1)S(1)} all-gather(bf16[160,128]{1,0:T(8,128)(2,1)S(1)} %get-tuple-element.53), channel_id=2, replica_groups=mesh['slab_0'=8,'slab_1'=4,'slab_2'=2,'tile'=8] {'slab_2'}, dimensions={0}, use_global_device_ids=true | all-gather | bytes 122880 | tf_op jit(solution)/shard_map/all_gather | solution.py:326
  18.6 0.0 collective-permute-done.2
  18.7 0.3 shard_map.93
  18.9 7.3 %all_to_all.20.stats_ref = f32[8,1,384]{2,1,0:T(1,128)S(1)} all-to-all(f32[8,1,384]{2,1,0:T(1,128)S(1)} %get-tuple-element.43), channel_id=1, replica_groups=mesh['slab_0'=8,'slab_1'=4,'slab_2'=2,'tile'=8] {'slab_1','slab_2'}, dimensions={0} | all-to-all | bytes 24576 | tf_op jit(solution)/shard_map/all_to_all | solution.py:341
  26.3 0.7 shard_map.95
  26.9 20.8 %all-to-all-start.1 = ((f32[64,1,384]{2,1,0:T(1,128)}), f32[64,1,384]{2,1,0:T(1,128)S(1)}, u32[]{:S(2)}, u32[]{:S(2)}) async-start(f32[64,1,384]{2,1,0:T(1,128)} %shard_map.95), calls=%async_computation.1 | async-start | bytes 196608 | tf_op jit(solution)/shard_map/all_to_all | solution.py:344
  47.8 0.5 shard_map.94
  48.3 10.9 %all-to-all-done.1.stats_ref = f32[64,1,384]{2,1,0:T(1,128)S(1)} async-done(((f32[64,1,384]{2,1,0:T(1,128)}), f32[64,1,384]{2,1,0:T(1,128)S(1)}, u32[]{:S(2)}, u32[]{:S(2)}) %all-to-all-start.1) | async-done | bytes 98336 | tf_op jit(solution)/shard_map/all_to_all | solution.py:344
  59.2 1.3 %shard_map.96 = (f32[512,128]{1,0:T(8,128)S(1)}, f32[8,1,384]{2,1,0:T(1,128)S(1)}) custom-call(s32[8,128]{1,0:T(8,128)S(1)} %get-tuple-element.28.meta_ref, f32[832,128]{1,0:T(8,128)S(1)} %get-tuple-element.36.first_ref, s32[32,512]{1,0:T(8,128)S(1)} %get-tuple-element.37.rank_ref, s32[512,128]{1,0:T(8,128)S(1)} %get-tuple-element.38.rank_t_ref, ...), custom_call_target="tpu_custom_call" | custom-call | tf_op jit(solution)/shard_map/pallas_call | solution.py:302
  60.5 9.0 %all_to_all.21.stats_ref = f32[8,1,384]{2,1,0:T(1,128)S(1)} all-to-all(f32[8,1,384]{2,1,0:T(1,128)S(1)} %get-tuple-element.48), channel_id=1, replica_groups=mesh['slab_0'=8,'slab_1'=4,'slab_2'=2,'tile'=8] {'slab_1','slab_2'}, dimensions={0} | all-to-all | bytes 24576 | tf_op jit(solution)/shard_map/all_to_all | solution.py:341
  69.6 15.1 %all_to_all.22.stats_ref = f32[64,1,384]{2,1,0:T(1,128)S(1)} all-to-all(f32[64,1,384]{2,1,0:T(1,128)S(1)} %shard_map.97), channel_id=1, replica_groups=mesh['slab_0'=8,'slab_1'=4,'slab_2'=2,'tile'=8] {'slab_0','tile'}, dimensions={0} | all-to-all | bytes 196608 | tf_op jit(solution)/shard_map/all_to_all | solution.py:344
  84.7 0.8 shard_map.98
  (5 shorter events, 0.1 us)
Async XLA Ops:
  3.3 5.4 %collective-permute-start.1 = (bf16[160,128]{1,0:T(8,128)(2,1)S(1)}, bf16[160,128]{1,0:T(8,128)(2,1)S(1)}, u32[]{:S(2)}, u32[]{:S(2)}) collective-permute-start(bf16[160,128]{1,0:T(8,128)(2,1)S(1)} %get-tuple-element.57), channel_id=1, source_target_pairs={{0,1},{1,0},{2,3},{3,2},{4,5},{5,4},{6,7},{7,6},{8,9},{9,8},{10,11... | collective-permute-start | bytes 122888 | tf_op jit(solution)/shard_map/ppermute | solution.py:335
  7.3 1.4 %collective-permute-start = (bf16[160,128]{1,0:T(8,128)(2,1)S(1)}, bf16[160,128]{1,0:T(8,128)(2,1)S(1)}, u32[]{:S(2)}, u32[]{:S(2)}) collective-permute-start(bf16[160,128]{1,0:T(8,128)(2,1)S(1)} %get-tuple-element.58), channel_id=1, source_target_pairs={{1,2},{3,4},{5,6},{2,1},{4,3},{6,5},{9,10},{11,12},{13,14},{10,9},... | collective-permute-start | bytes 122888 | tf_op jit(solution)/shard_map/ppermute | solution.py:336
  9.1 9.5 %collective-permute-start.2 = (bf16[160,128]{1,0:T(8,128)(2,1)S(1)}, bf16[160,128]{1,0:T(8,128)(2,1)S(1)}, u32[]{:S(2)}, u32[]{:S(2)}) collective-permute-start(bf16[160,128]{1,0:T(8,128)(2,1)S(1)} %get-tuple-element.54), channel_id=1, source_target_pairs={{8,16},{24,32},{40,48},{56,64},{72,80},{88,96},{104,112},{120,128}... | collective-permute-start | bytes 122888 | tf_op jit(solution)/shard_map/ppermute | solution.py:325
  26.9 32.3 %all-to-all-start.1 = ((f32[64,1,384]{2,1,0:T(1,128)}), f32[64,1,384]{2,1,0:T(1,128)S(1)}, u32[]{:S(2)}, u32[]{:S(2)}) async-start(f32[64,1,384]{2,1,0:T(1,128)} %shard_map.95), calls=%async_computation.1 | async-start | bytes 196608 | tf_op jit(solution)/shard_map/all_to_all | solution.py:344

commit v4 on v3

--- a/solution.py
+++ b/solution.py
@@ -163,7 +163,7 @@
         ref[...] = jnp.concatenate([*pieces, out_ref[far : far + SIDE_ROWS]], axis=0).astype(jnp.bfloat16)
 
 
-def tile_kernel(sums_ref, low_ref, high_ref, faces_ref, out_ref, left_ref, right_ref):
+def tile_kernel(sums_ref, low_ref, high_ref, slab_ref, tile_ref, out_ref, left_ref, right_ref):
     out_ref[...] = sums_ref[...]
     first, last = SIDE_ROWS + COLUMN, SIDE_ROWS + COLUMN + FACE
     low, high = low_ref[...].astype(jnp.float32), high_ref[...].astype(jnp.float32)
@@ -172,8 +172,8 @@
     for sent, at in ((low, 0), (high, FACE - COLUMN)):
         out_ref[A + at : A + at + COLUMN] += sent[SIDE_ROWS:first]
         out_ref[B + at : B + at + COLUMN] += sent[last:]
-    out_ref[:ROWS] += put(face_hot(faces_ref, 2), [low[first:last], high[first:last]])
-    picked = pick(face_hot(faces_ref, 0), out_ref[:ROWS])
+    out_ref[:ROWS] += put(tile_ref[...], [low[first:last], high[first:last]])
+    picked = pick(slab_ref[...], out_ref[:ROWS])
     for ref, own, own_at, far, far_at in (
         (left_ref, picked[:FACE], COLUMN, A, 0),
         (right_ref, picked[FACE:], FACE, B, FACE + COLUMN),
@@ -184,7 +184,7 @@
         ref[...] = jnp.concatenate(pieces, axis=0).astype(jnp.bfloat16)
 
 
-def slab_kernel(meta_ref, sums_ref, low_ref, high_ref, faces_ref, out_ref, stats_ref):
+def slab_kernel(meta_ref, sums_ref, low_ref, high_ref, slab_ref, out_ref, stats_ref):
     out_ref[...] = sums_ref[...]
     low, high = low_ref[...].astype(jnp.float32), high_ref[...].astype(jnp.float32)
     for sent, far, far_at, own_at in ((low, A, 0, COLUMN), (high, B, FACE + COLUMN, FACE)):
@@ -193,7 +193,7 @@
             out_ref[QH + at : QH + at + COLUMN] += sent[start + FACE : start + FACE + COLUMN]
             out_ref[QL + at : QL + at + COLUMN] += sent[start + FACE + COLUMN : start + SIDE_ROWS]
     own = slice(SIDE_ROWS, SIDE_ROWS + FACE)
-    total = out_ref[:ROWS] + put(face_hot(faces_ref, 0), [low[own], high[own]])
+    total = out_ref[:ROWS] + put(slab_ref[...], [low[own], high[own]])
     out_ref[:ROWS] = total
     write_sums(stats_ref, sums_of(total, meta_ref))
 
@@ -211,8 +211,9 @@
     return hot(jnp.bitwise_and(source, ROWS - 1), (total, ROWS), 1), jnp.broadcast_to(source, (total, CH))
 
 
-def source_kernel(rank_ref, digits_ref, hot_ref, source_ref, to_slot_ref):
+def source_kernel(rank_ref, digits_ref, faces_ref, hot_ref, source_ref, slab_ref, tile_ref, to_slot_ref):
     hot_ref[...], source_ref[...] = sources(0, rank_ref, digits_ref, to_slot_ref)
+    slab_ref[...], tile_ref[...] = face_hot(faces_ref, 0), face_hot(faces_ref, 2)
 
 
 def gather_kernel(
@@ -367,12 +368,14 @@
         spread_kernel, outs, scratch, 24, taps, features[0, 0], conv_one, face_rows[0, 0], *params, hbm=True
     )
     total = SIDES * SLOTS
-    outs = (shaped((total, ROWS), bf16), shaped((total, CH), i32))
+    outs = (shaped((total, ROWS), bf16), shaped((total, CH), i32), *(shaped((ROWS, 2 * FACE), bf16),) * 2)
     received = tile_neighbours(down, up)
-    source = call(source_kernel, outs, conv_scratch()[:1], 8, plan[0], plan[2])
-    first, left, right = call(tile_kernel, (ext, message, message), [], 8, first, *received, faces)
+    *source, at_slab, at_tile = call(
+        source_kernel, outs, conv_scratch()[:1], 8, plan[0], plan[2], faces
+    )
+    first, left, right = call(tile_kernel, (ext, message, message), [], 8, first, *received, at_slab, at_tile)
     received = slab_neighbours(left, right)
-    first, sums = call(slab_kernel, (ext, small), [], 8, meta, first, *received, faces)
+    first, sums = call(slab_kernel, (ext, small), [], 8, meta, first, *received, at_slab)
     stats = reduce_all(sums)
     second, sums = call(
         gather_kernel, (big, small), [pltpu.VMEM((ROWS, 2 * CH), bf16), *conv_scratch()], 24,

time: 85.8 us -> 84.8 us (0.988)
  blocking collectives: 36 us -> 68 us
  starting transfers between devices: 30.5 us -> 9.67 us
  waiting for transfers between devices: 11.6 us -> 0.14 us
    all_to_all x1 -> x2, blocking collectives: 15.1 us -> 47.1 us  [reduce_all(): return lax.all_to_all(block, ('slab_0', 'tile'), 0, 0)]
    all_to_all x1 -> x0, starting transfers between devices: 20.8 us -> none  [reduce_all(): return lax.all_to_all(block, ('slab_0', 'tile'), 0, 0)]
    all_to_all x1 -> x0, waiting for transfers between devices: 10.9 us -> none  [reduce_all(): return lax.all_to_all(block, ('slab_0', 'tile'), 0, 0)]
  transfers between devices with their start and end apart: 4 -> 3, of which waited for: 2 -> 1; matrix products, arithmetic and copies ran while one was open for 0% -> 0% of each run, Pallas kernels for 1% -> 1%
where the time goes in v4:
time: 84.8 us; the launch traced here: 84.5 us
  blocking collectives  68 us (80%)
  starting transfers between devices  9.67 us (11%)
  Pallas kernels  6.5 us (8%)
    all_to_all x2, blocking collectives, reduce_all(): return lax.all_to_all(block, ('slab_0', 'tile'), 0, 0)  47.1 us
    all_to_all x2, blocking collectives, reduce_all(): near = lax.all_to_all(sums, ('slab_1', 'slab_2'), 0, 0)  16.4 us
    pallas_call x8, Pallas kernels, call(): pl.pallas_call(kernel, out_shape=outs, in_specs=[pl.BlockSpec(memory_spac...  6.5 us
    ppermute x1, starting transfers between devices, slab_neighbours(): far = lax.ppermute(jnp.where(even, to_low, to_high), SLAB, across)  4.99 us
    all_gather x1, blocking collectives, slab_neighbours(): both = lax.all_gather(jnp.where(even, to_high, to_low), 'slab_2')  4.52 us
    ppermute x1, starting transfers between devices, tile_neighbours(): one = lax.ppermute(jnp.where(even, to_high, to_low), 'tile', inner)  4.02 us
  transfers between devices with their start and end apart: 3, of which 1 were waited for; matrix products, arithmetic and copies ran while one was open for 0% of the time, Pallas kernels for 1%

profile of v4, /device:TPU:1, one launch (start us, length us, event | category | flops | bytes accessed | tf_op | source)
XLA Modules:
  0.0 84.5 jit_solution(18313408386119662317)
XLA Ops:
  0.0 3.2 %shard_map.91 = (f32[832,128]{1,0:T(8,128)S(1)}, bf16[160,128]{1,0:T(8,128)(2,1)S(1)}, bf16[160,128]{1,0:T(8,128)(2,1)S(1)}, s32[32,512]{1,0:T(8,128)S(1)}, s32[...) custom-call(s32[27,1,512]{2,1,0:T(1,128)} %bitcast.9, ...), custom_call_target="tpu_custom_call" | custom-call | tf_op jit(solution)/shard_map/pallas_call | solution.py:303
  3.3 4.0 %collective-permute-start.1 = (bf16[160,128]{1,0:T(8,128)(2,1)S(1)}, bf16[160,128]{1,0:T(8,128)(2,1)S(1)}, u32[]{:S(2)}, u32[]{:S(2)}) collective-permute-start(bf16[160,128]{1,0:T(8,128)(2,1)S(1)} %get-tuple-element.61), channel_id=1, source_target_pairs={{0,1},{1,0},{2,3},{3,2},{4,5},{5,4},{6,7},{7,6},{8,9},{9,8},{10,11... | collective-permute-start | bytes 122888 | tf_op jit(solution)/shard_map/ppermute | solution.py:336
  7.3 0.7 collective-permute-start
  8.0 0.6 shard_map.92
  8.5 0.1 collective-permute-done.1
  8.7 0.0 collective-permute-done
  8.7 0.4 shard_map.93
  9.1 5.0 %collective-permute-start.2 = (bf16[160,128]{1,0:T(8,128)(2,1)S(1)}, bf16[160,128]{1,0:T(8,128)(2,1)S(1)}, u32[]{:S(2)}, u32[]{:S(2)}) collective-permute-start(bf16[160,128]{1,0:T(8,128)(2,1)S(1)} %get-tuple-element.58), channel_id=1, source_target_pairs={{8,16},{24,32},{40,48},{56,64},{72,80},{88,96},{104,112},{120,128}... | collective-permute-start | bytes 122888 | tf_op jit(solution)/shard_map/ppermute | solution.py:326
  14.1 4.5 %all-gather = bf16[320,128]{1,0:T(8,128)(2,1)S(1)} all-gather(bf16[160,128]{1,0:T(8,128)(2,1)S(1)} %get-tuple-element.57), channel_id=2, replica_groups=mesh['slab_0'=8,'slab_1'=4,'slab_2'=2,'tile'=8] {'slab_2'}, dimensions={0}, use_global_device_ids=true | all-gather | bytes 122880 | tf_op jit(solution)/shard_map/all_gather | solution.py:327
  18.6 0.0 collective-permute-done.2
  18.6 0.2 shard_map.94
  18.8 7.3 %all_to_all.20.stats_ref = f32[8,1,384]{2,1,0:T(1,128)S(1)} all-to-all(f32[8,1,384]{2,1,0:T(1,128)S(1)} %get-tuple-element.47), channel_id=1, replica_groups=mesh['slab_0'=8,'slab_1'=4,'slab_2'=2,'tile'=8] {'slab_1','slab_2'}, dimensions={0} | all-to-all | bytes 24576 | tf_op jit(solution)/shard_map/all_to_all | solution.py:342
  26.2 32.0 %all_to_all.21.stats_ref = f32[64,1,384]{2,1,0:T(1,128)S(1)} all-to-all(f32[64,1,384]{2,1,0:T(1,128)S(1)} %shard_map.95), channel_id=1, replica_groups=mesh['slab_0'=8,'slab_1'=4,'slab_2'=2,'tile'=8] {'slab_0','tile'}, dimensions={0} | all-to-all | bytes 196608 | tf_op jit(solution)/shard_map/all_to_all | solution.py:345
  58.2 1.3 %shard_map.96 = (f32[512,128]{1,0:T(8,128)S(1)}, f32[8,1,384]{2,1,0:T(1,128)S(1)}) custom-call(s32[8,128]{1,0:T(8,128)S(1)} %get-tuple-element.30.meta_ref, f32[832,128]{1,0:T(8,128)S(1)} %get-tuple-element.42.first_ref, s32[32,512]{1,0:T(8,128)S(1)} %get-tuple-element.34.rank_ref, s32[512,128]{1,0:T(8,128)S(1)} %get-tuple-element.43.rank_t_ref, ...), custom_call_target="tpu_custom_call" | custom-call | tf_op jit(solution)/shard_map/pallas_call | solution.py:303
  59.6 9.0 %all_to_all.22.stats_ref = f32[8,1,384]{2,1,0:T(1,128)S(1)} all-to-all(f32[8,1,384]{2,1,0:T(1,128)S(1)} %get-tuple-element.52), channel_id=1, replica_groups=mesh['slab_0'=8,'slab_1'=4,'slab_2'=2,'tile'=8] {'slab_1','slab_2'}, dimensions={0} | all-to-all | bytes 24576 | tf_op jit(solution)/shard_map/all_to_all | solution.py:342
  68.6 15.1 %all_to_all.23.stats_ref = f32[64,1,384]{2,1,0:T(1,128)S(1)} all-to-all(f32[64,1,384]{2,1,0:T(1,128)S(1)} %shard_map.97), channel_id=1, replica_groups=mesh['slab_0'=8,'slab_1'=4,'slab_2'=2,'tile'=8] {'slab_0','tile'}, dimensions={0} | all-to-all | bytes 196608 | tf_op jit(solution)/shard_map/all_to_all | solution.py:345
  83.7 0.8 shard_map.98
  (6 shorter events, 0.1 us)
Async XLA Ops:
  3.3 5.4 %collective-permute-start.1 = (bf16[160,128]{1,0:T(8,128)(2,1)S(1)}, bf16[160,128]{1,0:T(8,128)(2,1)S(1)}, u32[]{:S(2)}, u32[]{:S(2)}) collective-permute-start(bf16[160,128]{1,0:T(8,128)(2,1)S(1)} %get-tuple-element.61), channel_id=1, source_target_pairs={{0,1},{1,0},{2,3},{3,2},{4,5},{5,4},{6,7},{7,6},{8,9},{9,8},{10,11... | collective-permute-start | bytes 122888 | tf_op jit(solution)/shard_map/ppermute | solution.py:336
  7.3 1.4 %collective-permute-start = (bf16[160,128]{1,0:T(8,128)(2,1)S(1)}, bf16[160,128]{1,0:T(8,128)(2,1)S(1)}, u32[]{:S(2)}, u32[]{:S(2)}) collective-permute-start(bf16[160,128]{1,0:T(8,128)(2,1)S(1)} %get-tuple-element.62), channel_id=1, source_target_pairs={{1,2},{3,4},{5,6},{2,1},{4,3},{6,5},{9,10},{11,12},{13,14},{10,9},... | collective-permute-start | bytes 122888 | tf_op jit(solution)/shard_map/ppermute | solution.py:337
  9.1 9.5 %collective-permute-start.2 = (bf16[160,128]{1,0:T(8,128)(2,1)S(1)}, bf16[160,128]{1,0:T(8,128)(2,1)S(1)}, u32[]{:S(2)}, u32[]{:S(2)}) collective-permute-start(bf16[160,128]{1,0:T(8,128)(2,1)S(1)} %get-tuple-element.58), channel_id=1, source_target_pairs={{8,16},{24,32},{40,48},{56,64},{72,80},{88,96},{104,112},{120,128}... | collective-permute-start | bytes 122888 | tf_op jit(solution)/shard_map/ppermute | solution.py:326

commit v5 on v4

--- a/solution.py
+++ b/solution.py
@@ -289,14 +289,22 @@
     return (values - average) * scale + shift
 
 
-def finish_kernel(meta_ref, second_ref, rows_ref, stats_ref, gain_ref, shift_ref, out_ref):
-    stats = total_of(stats_ref)
-    norm = scale_of(stats, gain_ref[...], shift_ref[...])
-    summed = affine(second_ref[...], *norm) + rows_ref[...].astype(jnp.float32)
-    out_ref[...] = (live_rows(meta_ref) * jnp.maximum(summed, 0.0)).astype(jnp.bfloat16)
-
-
-def call(kernel, outs, scratch, limit, *args, hbm=False):
+def finish_kernel(meta_ref, second_ref, rows_ref, stats_ref, gain_ref, shift_ref, out_hbm, out_ref, sems):
+    norm = scale_of(total_of(stats_ref), gain_ref[...], shift_ref[...])
+    live = live_rows(meta_ref)
+    size = ROWS // 4
+    copies = []
+    for i in range(4):
+        at = slice(i * size, (i + 1) * size)
+        summed = affine(second_ref[at], *norm) + rows_ref[at].astype(jnp.float32)
+        out_ref[at] = (live[at] * jnp.maximum(summed, 0.0)).astype(jnp.bfloat16)
+        copies += [pltpu.make_async_copy(out_ref.at[pl.ds(i * size, size)], out_hbm.at[pl.ds(i * size, size)], sems.at[i])]
+        copies[-1].start()
+    for copy in copies:
+        copy.wait()
+
+
+def call(kernel, outs, scratch, limit, *args, hbm=False, out_hbm=False):
     vmem = pl.BlockSpec(memory_space=pltpu.VMEM)
     if hbm:
         args = [pltpu.with_memory_space_constraint(a, pltpu.HBM) for a in args]
@@ -304,7 +312,7 @@
         kernel,
         out_shape=outs,
         in_specs=[pl.BlockSpec(memory_space=pltpu.HBM) if hbm else vmem] * len(args),
-        out_specs=jax.tree.map(lambda _: vmem, outs),
+        out_specs=jax.tree.map(lambda _: pl.BlockSpec(memory_space=pltpu.HBM) if out_hbm else vmem, outs),
         scratch_shapes=scratch,
         compiler_params=pltpu.CompilerParams(vmem_limit_bytes=limit << 20),
     )(*args)
@@ -383,7 +391,9 @@
     )
     stats = reduce_all(sums)
     out = call(
-        finish_kernel, shaped((ROWS, CH), bf16), [], 4, meta, second, rows, stats, gain_two, shift_two
+        finish_kernel, shaped((ROWS, CH), bf16),
+        [pltpu.VMEM((ROWS, CH), bf16), pltpu.SemaphoreType.DMA((4,))], 4,
+        meta, second, rows, stats, gain_two, shift_two, out_hbm=True,
     )
     return out[None, None]
 

time: 84.8 us -> 84.8 us (level)
  no operation moved by 1% of the time
where the time goes in v5:
time: 84.8 us; the launch traced here: 84.5 us
  blocking collectives  68 us (80%)
  starting transfers between devices  9.67 us (11%)
  Pallas kernels  6.5 us (8%)
    all_to_all x2, blocking collectives, reduce_all(): return lax.all_to_all(block, ('slab_0', 'tile'), 0, 0)  47.1 us
    all_to_all x2, blocking collectives, reduce_all(): near = lax.all_to_all(sums, ('slab_1', 'slab_2'), 0, 0)  16.4 us
    pallas_call x8, Pallas kernels, call(): pl.pallas_call(kernel, out_shape=outs, in_specs=[pl.BlockSpec(memory_spac...  6.5 us
    ppermute x1, starting transfers between devices, slab_neighbours(): far = lax.ppermute(jnp.where(even, to_low, to_high), SLAB, across)  4.99 us
    all_gather x1, blocking collectives, slab_neighbours(): both = lax.all_gather(jnp.where(even, to_high, to_low), 'slab_2')  4.52 us
    ppermute x1, starting transfers between devices, tile_neighbours(): one = lax.ppermute(jnp.where(even, to_high, to_low), 'tile', inner)  4.02 us
  transfers between devices with their start and end apart: 3, of which 1 were waited for; matrix products, arithmetic and copies ran while one was open for 0% of the time, Pallas kernels for 1%

profile of v5, /device:TPU:1, one launch (start us, length us, event | category | flops | bytes accessed | tf_op | source)
XLA Modules:
  0.0 84.5 jit_solution(12018796794924080055)
XLA Ops:
  0.0 3.2 %shard_map.91 = (f32[832,128]{1,0:T(8,128)S(1)}, bf16[160,128]{1,0:T(8,128)(2,1)S(1)}, bf16[160,128]{1,0:T(8,128)(2,1)S(1)}, s32[32,512]{1,0:T(8,128)S(1)}, s32[...) custom-call(s32[27,1,512]{2,1,0:T(1,128)} %bitcast.9, ...), custom_call_target="tpu_custom_call" | custom-call | tf_op jit(solution)/shard_map/pallas_call | solution.py:311
  3.3 4.0 %collective-permute-start.1 = (bf16[160,128]{1,0:T(8,128)(2,1)S(1)}, bf16[160,128]{1,0:T(8,128)(2,1)S(1)}, u32[]{:S(2)}, u32[]{:S(2)}) collective-permute-start(bf16[160,128]{1,0:T(8,128)(2,1)S(1)} %get-tuple-element.61), channel_id=1, source_target_pairs={{0,1},{1,0},{2,3},{3,2},{4,5},{5,4},{6,7},{7,6},{8,9},{9,8},{10,11... | collective-permute-start | bytes 122888 | tf_op jit(solution)/shard_map/ppermute | solution.py:344
  7.3 0.7 collective-permute-start
  8.0 0.6 shard_map.92
  8.5 0.1 collective-permute-done.1
  8.7 0.0 collective-permute-done
  8.7 0.4 shard_map.93
  9.1 5.0 %collective-permute-start.2 = (bf16[160,128]{1,0:T(8,128)(2,1)S(1)}, bf16[160,128]{1,0:T(8,128)(2,1)S(1)}, u32[]{:S(2)}, u32[]{:S(2)}) collective-permute-start(bf16[160,128]{1,0:T(8,128)(2,1)S(1)} %get-tuple-element.58), channel_id=1, source_target_pairs={{8,16},{24,32},{40,48},{56,64},{72,80},{88,96},{104,112},{120,128}... | collective-permute-start | bytes 122888 | tf_op jit(solution)/shard_map/ppermute | solution.py:334
  14.1 4.5 %all-gather = bf16[320,128]{1,0:T(8,128)(2,1)S(1)} all-gather(bf16[160,128]{1,0:T(8,128)(2,1)S(1)} %get-tuple-element.57), channel_id=2, replica_groups=mesh['slab_0'=8,'slab_1'=4,'slab_2'=2,'tile'=8] {'slab_2'}, dimensions={0}, use_global_device_ids=true | all-gather | bytes 122880 | tf_op jit(solution)/shard_map/all_gather | solution.py:335
  18.6 0.0 collective-permute-done.2
  18.6 0.2 shard_map.94
  18.8 7.3 %all_to_all.20.stats_ref = f32[8,1,384]{2,1,0:T(1,128)S(1)} all-to-all(f32[8,1,384]{2,1,0:T(1,128)S(1)} %get-tuple-element.47), channel_id=1, replica_groups=mesh['slab_0'=8,'slab_1'=4,'slab_2'=2,'tile'=8] {'slab_1','slab_2'}, dimensions={0} | all-to-all | bytes 24576 | tf_op jit(solution)/shard_map/all_to_all | solution.py:350
  26.2 32.0 %all_to_all.21.stats_ref = f32[64,1,384]{2,1,0:T(1,128)S(1)} all-to-all(f32[64,1,384]{2,1,0:T(1,128)S(1)} %shard_map.95), channel_id=1, replica_groups=mesh['slab_0'=8,'slab_1'=4,'slab_2'=2,'tile'=8] {'slab_0','tile'}, dimensions={0} | all-to-all | bytes 196608 | tf_op jit(solution)/shard_map/all_to_all | solution.py:353
  58.2 1.3 %shard_map.96 = (f32[512,128]{1,0:T(8,128)S(1)}, f32[8,1,384]{2,1,0:T(1,128)S(1)}) custom-call(s32[8,128]{1,0:T(8,128)S(1)} %get-tuple-element.30.meta_ref, f32[832,128]{1,0:T(8,128)S(1)} %get-tuple-element.42.first_ref, s32[32,512]{1,0:T(8,128)S(1)} %get-tuple-element.34.rank_ref, s32[512,128]{1,0:T(8,128)S(1)} %get-tuple-element.43.rank_t_ref, ...), custom_call_target="tpu_custom_call" | custom-call | tf_op jit(solution)/shard_map/pallas_call | solution.py:311
  59.6 9.0 %all_to_all.22.stats_ref = f32[8,1,384]{2,1,0:T(1,128)S(1)} all-to-all(f32[8,1,384]{2,1,0:T(1,128)S(1)} %get-tuple-element.52), channel_id=1, replica_groups=mesh['slab_0'=8,'slab_1'=4,'slab_2'=2,'tile'=8] {'slab_1','slab_2'}, dimensions={0} | all-to-all | bytes 24576 | tf_op jit(solution)/shard_map/all_to_all | solution.py:350
  68.6 15.1 %all_to_all.23.stats_ref = f32[64,1,384]{2,1,0:T(1,128)S(1)} all-to-all(f32[64,1,384]{2,1,0:T(1,128)S(1)} %shard_map.97), channel_id=1, replica_groups=mesh['slab_0'=8,'slab_1'=4,'slab_2'=2,'tile'=8] {'slab_0','tile'}, dimensions={0} | all-to-all | bytes 196608 | tf_op jit(solution)/shard_map/all_to_all | solution.py:353
  83.7 0.8 shard_map.98
  (6 shorter events, 0.1 us)
Async XLA Ops:
  3.3 5.4 %collective-permute-start.1 = (bf16[160,128]{1,0:T(8,128)(2,1)S(1)}, bf16[160,128]{1,0:T(8,128)(2,1)S(1)}, u32[]{:S(2)}, u32[]{:S(2)}) collective-permute-start(bf16[160,128]{1,0:T(8,128)(2,1)S(1)} %get-tuple-element.61), channel_id=1, source_target_pairs={{0,1},{1,0},{2,3},{3,2},{4,5},{5,4},{6,7},{7,6},{8,9},{9,8},{10,11... | collective-permute-start | bytes 122888 | tf_op jit(solution)/shard_map/ppermute | solution.py:344
  7.3 1.4 %collective-permute-start = (bf16[160,128]{1,0:T(8,128)(2,1)S(1)}, bf16[160,128]{1,0:T(8,128)(2,1)S(1)}, u32[]{:S(2)}, u32[]{:S(2)}) collective-permute-start(bf16[160,128]{1,0:T(8,128)(2,1)S(1)} %get-tuple-element.62), channel_id=1, source_target_pairs={{1,2},{3,4},{5,6},{2,1},{4,3},{6,5},{9,10},{11,12},{13,14},{10,9},... | collective-permute-start | bytes 122888 | tf_op jit(solution)/shard_map/ppermute | solution.py:345
  9.1 9.5 %collective-permute-start.2 = (bf16[160,128]{1,0:T(8,128)(2,1)S(1)}, bf16[160,128]{1,0:T(8,128)(2,1)S(1)}, u32[]{:S(2)}, u32[]{:S(2)}) collective-permute-start(bf16[160,128]{1,0:T(8,128)(2,1)S(1)} %get-tuple-element.58), channel_id=1, source_target_pairs={{8,16},{24,32},{40,48},{56,64},{72,80},{88,96},{104,112},{120,128}... | collective-permute-start | bytes 122888 | tf_op jit(solution)/shard_map/ppermute | solution.py:334
